TPU v7x, 32 devices: a whole 2x2x4 slice. The times are simulated.
32 devices in a mesh: groups: 2 (over x), sp: 8 (over z, y), fsdp: 2 (over core).
Axes of the slice: x: 2, y: 2, z: 4, core: 2. Of those that a mesh axis runs over, the one named last changes fastest.
Arguments:
- policy_hidden: bfloat16 [4, 256, 4096], P(('groups', 'fsdp'), 'sp'), parts along dimension 0, may hold values from -6 to 6
- policy_queries: bfloat16 [4, 256, 1024], P(('groups', 'fsdp'), 'sp'), parts along dimension 0, may hold values from -512 to 512
- policy_documents: int32 [4, 256], P(('groups', 'fsdp'), 'sp'), parts along dimension 0, may hold values from 0 to 31, never falling along the last dimension, each value on 1 to 128 neighbouring positions
- policy_gain: bfloat16 [4096], P(('sp', 'fsdp')), may hold values from 0.099609375 to 1.8984375
- policy_key_weight: bfloat16 [4096, 512], P(('sp', 'fsdp')), may hold values from -0.09375 to 0.09375
- policy_value_weight: bfloat16 [4096, 512], P(('sp', 'fsdp')), may hold values from -0.09375 to 0.09375
- frozen_hidden: bfloat16 [4, 256, 4096], P(('groups', 'fsdp'), 'sp'), parts along dimension 0, may hold values from -6 to 6
- frozen_queries: bfloat16 [4, 256, 1024], P(('groups', 'fsdp'), 'sp'), parts along dimension 0, may hold values from -512 to 512
- frozen_documents: int32 [4, 256], P(('groups', 'fsdp'), 'sp'), parts along dimension 0, may hold values from 0 to 31, never falling along the last dimension, each value on 1 to 128 neighbouring positions
- frozen_gain: bfloat16 [4096], P(('sp', 'fsdp')), may hold values from 0.099609375 to 1.8984375
- frozen_key_weight: bfloat16 [4096, 512], P(('sp', 'fsdp')), may hold values from -0.09375 to 0.09375
- frozen_value_weight: bfloat16 [4096, 512], P(('sp', 'fsdp')), may hold values from -0.09375 to 0.09375
Outputs:
- policy_mixed: bfloat16 [4, 256, 1024], P(('groups', 'fsdp'), 'sp'), parts along dimension 0
- frozen_mixed: bfloat16 [4, 256, 1024], P(('groups', 'fsdp'), 'sp'), parts along dimension 0
There are 2 independent parts, one for each index of `groups`. A program takes and returns all parts, laid end to end along the dimension named above; an argument that names none is the same for every part. Nothing has to cross between parts.
Inputs may be any that keep to these rules, and one draw needn't show every extreme that they name: `policy_documents`: along each sequence the ids never fall, and each document holds 1 to 128 positions. `frozen_documents`: along each sequence the ids never fall, and each document holds 1 to 128 positions.
All inputs are finite; a program needn't handle non-finite values.
Results may differ from a plain program's by a relative error of at most 0.007.
The roundings to bfloat16 on the way count: a program that leaves them out, or rounds other values in their place, can miss the bound.
Values may be sent and summed in bfloat16 or wider, within the bound.
A program may use at most 128 MiB of HBM per device.

v0:
```python
import functools

import jax
import jax.numpy as jnp
import numpy as np
from jax import lax
from jax.experimental import pallas as pl
from jax.experimental.pallas import tpu as pltpu
from jax.sharding import PartitionSpec as P

HEAD_DIM = 128
LAG = 2


EPS = 1e-05
ROPE_BASE = 500000.0
MASKED = -1e30


def rotate(raw_keys, positions):
    half_dim = HEAD_DIM // 2
    frequency = jnp.exp(
        -jnp.log(ROPE_BASE) * jnp.arange(half_dim, dtype=jnp.float32) * 2.0 / HEAD_DIM
    )
    angles = positions.astype(jnp.float32)[:, None] * frequency[None, :]
    cosines = jnp.cos(angles)[:, None, :]
    sines = jnp.sin(angles)[:, None, :]
    front_half = raw_keys[..., :half_dim]
    back_half = raw_keys[..., half_dim:]
    return jnp.concatenate(
        [front_half * cosines - back_half * sines, back_half * cosines + front_half * sines],
        axis=-1,
    )


def project(hidden, gain, key_weight, value_weight):
    tokens = hidden.shape[1]
    widened = hidden[0].astype(jnp.float32)
    inverse = lax.rsqrt(jnp.mean(widened * widened, axis=-1, keepdims=True) + EPS)
    scaled = widened * inverse
    gain_rows = lax.all_gather(gain, ("sp", "fsdp"), axis=0, tiled=True)
    key_rows = lax.all_gather(key_weight, ("sp", "fsdp"), axis=0, tiled=True)
    value_rows = lax.all_gather(value_weight, ("sp", "fsdp"), axis=0, tiled=True)
    normed = (scaled * gain_rows.astype(jnp.float32)[None, :]).astype(jnp.bfloat16)
    raw_keys = jnp.dot(normed, key_rows, preferred_element_type=jnp.float32)
    raw_values = jnp.dot(normed, value_rows, preferred_element_type=jnp.float32)
    positions = lax.axis_index("sp") * tokens + jnp.arange(tokens, dtype=jnp.int32)
    key_heads = rotate(raw_keys.reshape(tokens, -1, HEAD_DIM), positions).astype(jnp.bfloat16)
    value_heads = raw_values.astype(jnp.bfloat16).reshape(tokens, -1, HEAD_DIM)
    return (key_heads, value_heads)


def attend(queries, key_heads, value_heads, documents):
    length = queries.shape[0]
    head_count = queries.shape[1]
    block_rows = min(512, length)
    margin = min(512, length // 2)
    window = block_rows + margin
    factor = HEAD_DIM ** (-0.5)
    offsets = jnp.arange(block_rows, dtype=jnp.int32)
    window_offsets = jnp.arange(window, dtype=jnp.int32)
    padding = jnp.zeros((margin, head_count, HEAD_DIM), jnp.bfloat16)
    padded_keys = jnp.concatenate([padding, key_heads], axis=0)
    padded_values = jnp.concatenate([padding, value_heads], axis=0)
    padded_docs = jnp.concatenate([jnp.full((margin,), -1, jnp.int32), documents], axis=0)

    def one_block(block_index):
        first = block_index * block_rows
        query_block = lax.dynamic_slice_in_dim(queries, first, block_rows, 0)
        query_docs = lax.dynamic_slice_in_dim(documents, first, block_rows, 0)
        query_positions = first + offsets
        key_block = lax.dynamic_slice_in_dim(padded_keys, first, window, 0)
        value_block = lax.dynamic_slice_in_dim(padded_values, first, window, 0)
        key_docs = lax.dynamic_slice_in_dim(padded_docs, first, window, 0)
        key_positions = first - margin + window_offsets
        allowed = (key_positions[None, :] <= query_positions[:, None]) & (
            key_docs[None, :] == query_docs[:, None]
        )
        scores = (
            jnp.einsum("qnd,knd->nqk", query_block, key_block, preferred_element_type=jnp.float32)
            * factor
        )
        scores = jnp.where(allowed[None], scores, MASKED)
        highest = jnp.max(scores, axis=-1, keepdims=True)
        exponent = jnp.where(allowed[None], jnp.exp(scores - highest), 0.0)
        weights = (exponent / jnp.sum(exponent, axis=-1, keepdims=True)).astype(jnp.bfloat16)
        blended = jnp.einsum(
            "nqk,knd->qnd", weights, value_block, preferred_element_type=jnp.float32
        )
        return blended.astype(jnp.bfloat16)

    blocks = lax.map(one_block, jnp.arange(length // block_rows, dtype=jnp.int32))
    return blocks.reshape(length, head_count, HEAD_DIM)


def run_model(hidden, queries, documents, gain, key_weight, value_weight):
    tokens = hidden.shape[1]
    head_count = queries.shape[2] // HEAD_DIM
    query_local = queries[0].reshape(tokens, head_count, HEAD_DIM)
    every_doc = lax.all_gather(documents[0], "sp", axis=0, tiled=True)
    key_heads, value_heads = project(hidden, gain, key_weight, value_weight)
    group_size = head_count // key_heads.shape[1]
    wide_keys = jnp.repeat(key_heads, group_size, axis=1)
    wide_values = jnp.repeat(value_heads, group_size, axis=1)
    query_spread, key_spread, value_spread = (
        lax.all_to_all(query_local, "sp", split_axis=1, concat_axis=0, tiled=True),
        lax.all_to_all(wide_keys, "sp", split_axis=1, concat_axis=0, tiled=True),
        lax.all_to_all(wide_values, "sp", split_axis=1, concat_axis=0, tiled=True),
    )
    mixed = attend(query_spread, key_spread, value_spread, every_doc)
    returned = lax.all_to_all(mixed, "sp", split_axis=0, concat_axis=1, tiled=True)
    return returned.reshape(1, tokens, head_count * HEAD_DIM)


MESH = pl.DeviceIdType.MESH


def fits(mesh, hidden, queries, key_weight):
    sp, cores = mesh.shape["sp"], mesh.shape["fsdp"]
    tokens = hidden.shape[1]
    kv_heads = key_weight.shape[1] // HEAD_DIM
    return (
        cores == 2
        and mesh.shape["groups"] == 2
        and sp % 2 == 0
        and kv_heads % 2 == 0
        and kv_heads == 4
        and sp // 2 == cores * (kv_heads // 2)
        and queries.shape[2] % (kv_heads * HEAD_DIM) == 0
        and key_weight.shape[0] % 128 == 0
        and hidden.shape[2] == key_weight.shape[0] * sp * cores
        and tokens % 16 == 0
        and tokens <= 128
    )


def fused_kernel(
    sp_count,
    hidden0, hidden1, queries0, queries1, key0, key1, value0, value1,
    gain0, gain1, documents0, documents1, cosines, sines,
    out0, out1,
    near, near_sem, rows, wide_k, wide_v, gains, documents, gain_rows, norm_send, norm_rows, query_rows, doc_rows,
    part_send, relayed, parts, doc_wide, mixed,
    send_sem, hid_sem, fwd_sem, w_sem, gain_sem, norm_sem, q_sem, doc_sem, part_sem, relay_sem, out_sem,
):
    hiddens, queries = (hidden0, hidden1), (queries0, queries1)
    keys, values = (key0, key1), (value0, value1)
    tokens, features = hidden0.shape[1], key0.shape[0]
    slab = 4 * features
    half = key0.shape[1] // 2
    per_half = half // HEAD_DIM
    head_cols = query_rows.shape[1]
    length = query_rows.shape[0]
    layers = sp_count // 2
    sp, core = lax.axis_index("sp"), lax.axis_index("fsdp")
    z, y = sp // 2, sp % 2
    group = lax.axis_index("groups")
    me = sp * 2 + core
    total = sp_count * 2

    for m in range(2):
        pltpu.make_async_copy(hiddens[m].at[0], near.at[m], near_sem.at[m]).start()
    barrier = pltpu.get_barrier_semaphore()
    for step in range(1, total):
        other = lax.rem(me + step, total)
        pl.semaphore_signal(
            barrier, inc=1, device_id={"sp": other // 2, "fsdp": other % 2}, device_id_type=MESH
        )

    pl.semaphore_signal(barrier, inc=1, device_id={"groups": 1 - group}, device_id_type=MESH)

    square = (
        lax.broadcasted_iota(jnp.int32, (tokens, 128), 0)
        == lax.broadcasted_iota(jnp.int32, (tokens, 128), 1)
    )
    for m in range(2):
        pltpu.make_async_copy(hiddens[m].at[0], near.at[m], near_sem.at[m]).wait()
        wide = near[m].astype(jnp.float32)
        inverse = lax.rsqrt(jnp.mean(wide * wide, axis=-1, keepdims=True) + EPS)
        gains[m] = (gain0, gain1)[m][...].astype(jnp.float32).reshape(1, -1)
        documents[m] = jnp.zeros((1, 128), jnp.float32)
        documents[m, :, :tokens] = (documents0, documents1)[m][...].astype(jnp.float32)
        norm_send[m] = jnp.sum(jnp.where(square, inverse, 0.0), axis=0, keepdims=True)

    pl.semaphore_wait(barrier, total)

    pending = []

    def remote(src, dst, recv, target):
        slot = len(pending)

        def make():
            return pltpu.make_async_remote_copy(
                src_ref=src, dst_ref=dst, send_sem=send_sem.at[slot], recv_sem=recv,
                device_id=target, device_id_type=MESH,
            )

        return make

    def put(src, dst, recv, target, away):
        make = remote(src, dst, recv, target)
        pending.append((away, make))
        if away is None:
            make().start()
        else:
            @pl.when(away)
            def _():
                make().start()

    def send(src, dst, recv, to_sp, to_core, own):
        put(src, dst, recv, {"sp": to_sp, "fsdp": to_core}, None if own is None else jnp.logical_not(own))
        if own is not None:
            @pl.when(own)
            def _():
                pltpu.make_async_copy(src, dst, recv).start()

    def arrive(dst, recv):
        pltpu.make_async_copy(dst, dst, recv).wait()

    for dz in range(layers):
        to_z = lax.rem(z + dz, layers)
        for m in range(2):
            send(
                hiddens[m].at[0, :, pl.ds(pl.multiple_of(to_z * slab, 128), slab)],
                rows.at[sp, pl.ds(pl.multiple_of(core * tokens, 16), tokens)],
                hid_sem.at[z, core],
                to_z * 2 + y, m,
                (core == m) if dz == 0 else None,
            )
    place = pl.ds(pl.multiple_of((y * 2 + core) * features, 128), features)
    for dy in (1, 0):
        to_y = (y + dy) % 2
        columns = pl.ds(pl.multiple_of(to_y * half, 128), half)
        for m in range(2):
            own = (core == m) if dy == 0 else None
            if dy:
                target = {"sp": z * 2 + to_y, "fsdp": m}
                put(keys[m].at[:, columns], wide_k.at[place], w_sem.at[y * 2 + core, 0], target, core == group)
                put(values[m].at[:, columns], wide_v.at[place], w_sem.at[y * 2 + core, 1], target, core == group)
            else:
                send(keys[m].at[:, columns], wide_k.at[place], w_sem.at[y * 2 + core, 0], z * 2 + to_y, m, own)
                send(values[m].at[:, columns], wide_v.at[place], w_sem.at[y * 2 + core, 1], z * 2 + to_y, m, own)
            send(gains.at[m], gain_rows.at[y * 2 + core], gain_sem.at[y * 2 + core], z * 2 + to_y, m, own)
    for dz in range(layers):
        for dy in range(2):
            to_sp = lax.rem(z + dz, layers) * 2 + (y + dy) % 2
            for m in range(2):
                send(
                    norm_send.at[m], norm_rows.at[me], norm_sem.at[me], to_sp, m,
                    (core == m) if dz == 0 and dy == 0 else None,
                )
    token_rows = pl.ds(pl.multiple_of(sp * tokens, 16), tokens)
    for b in range(per_half):
        for to_y in range(2):
            head = to_y * per_half + b
            to_sp = (core * per_half + b) * 2 + to_y
            for m in range(2):
                own = (to_sp == sp) & (core == m)
                send(
                    queries[m].at[0, :, head * head_cols:(head + 1) * head_cols],
                    query_rows.at[token_rows], q_sem.at[sp], to_sp, m, own,
                )
                send(documents.at[m], doc_rows.at[sp], doc_sem.at[sp], to_sp, m, own)

    for dz in range(layers):
        from_z = lax.rem(z - dz + layers, layers)
        block = from_z * 2 + y
        for c in range(2):
            arrive(rows.at[block, c * tokens:(c + 1) * tokens], hid_sem.at[from_z, c])
        send(rows.at[block], rows.at[block], fwd_sem.at[from_z], z * 2 + (1 - y), core, None)
        if dz < 2:
            source = (1 - y) * 2 + group
            wide = (wide_k, wide_v)[dz].at[pl.ds(pl.multiple_of(source * features, 128), features)]
            arrive(wide, w_sem.at[source, dz])
            put(wide, wide, w_sem.at[source, dz], {"groups": 1 - group}, None)

    for s in range(total):
        arrive(norm_rows.at[s], norm_sem.at[s])
    for s in range(4):
        arrive(gain_rows.at[s], gain_sem.at[s])
    for source in (y * 2, y * 2 + 1, (1 - y) * 2 + 1 - group):
        place = pl.ds(pl.multiple_of(source * features, 128), features)
        arrive(wide_k.at[place], w_sem.at[source, 0])
        arrive(wide_v.at[place], w_sem.at[source, 1])
    gain_row = jnp.concatenate([gain_rows[s] for s in range(4)], axis=1)

    inner = (z == per_half - 1) | (z == per_half)
    outer = jnp.logical_not(inner)
    neighbour = per_half - 1 + z // per_half

    def onward(index):
        block = (index % layers) * 2 + (y + index // layers) % 2
        block_rows = pl.ds(pl.multiple_of(block * tokens, 16), tokens)
        for to_z in range(layers):
            slot = index * layers + to_z
            away = inner & (z // per_half != to_z // per_half)

            @pl.when(away)
            def _(slot=slot):
                arrive(relayed.at[slot], relay_sem.at[slot])
                part_send[slot] = part_send[slot] + relayed[slot]

            put(
                part_send.at[slot], parts.at[z, block_rows], part_sem.at[z, block],
                {"sp": to_z * 2 + y, "fsdp": core}, away,
            )

    for index in range(2 * layers):
        from_z, side = index % layers, index // layers
        block = from_z * 2 + (y + side) % 2
        if side:
            arrive(rows.at[block], fwd_sem.at[from_z])
        scale = jnp.concatenate(
            [
                jnp.sum(jnp.where(square, norm_rows[block * 2 + c], 0.0), axis=1, keepdims=True)
                for c in range(2)
            ],
            axis=0,
        )
        normed = (rows[block].astype(jnp.float32) * scale * gain_row).astype(jnp.bfloat16)
        part_k = jnp.dot(normed, wide_k[...], preferred_element_type=jnp.float32)
        part_v = jnp.dot(normed, wide_v[...], preferred_element_type=jnp.float32)
        block_rows = pl.ds(pl.multiple_of(block * tokens, 16), tokens)
        for s in range(2):
            for b in range(per_half):
                to_z = s * per_half + b
                same = z // per_half == s
                picked = (slice(s * tokens, (s + 1) * tokens), slice(b * HEAD_DIM, (b + 1) * HEAD_DIM))
                slot = index * layers + to_z
                part_send[slot, :, :HEAD_DIM] = part_k[picked]
                part_send[slot, :, HEAD_DIM:] = part_v[picked]
                put(
                    part_send.at[slot], parts.at[z, block_rows], part_sem.at[z, block],
                    {"sp": to_z * 2 + y, "fsdp": core}, same & (z != to_z),
                )
                put(
                    part_send.at[slot], relayed.at[slot], relay_sem.at[slot],
                    {"sp": neighbour * 2 + y, "fsdp": core}, outer & jnp.logical_not(same),
                )

                @pl.when(z == to_z)
                def _(slot=slot, block_rows=block_rows):
                    parts[z, block_rows, :] = part_send[slot]

        if index >= LAG:
            onward(index - LAG)
    for index in range(2 * layers - LAG, 2 * layers):
        onward(index)

    for s in range(sp_count):
        arrive(query_rows.at[s * tokens:(s + 1) * tokens], q_sem.at[s])
        arrive(doc_rows.at[s], doc_sem.at[s])
        column = jnp.sum(jnp.where(square, doc_rows[s], 0.0), axis=1, keepdims=True)
        doc_wide[s * tokens:(s + 1) * tokens, :] = jnp.broadcast_to(column, (tokens, 128))
    query_index = lax.broadcasted_iota(jnp.int32, (length, length), 0)
    key_index = lax.broadcasted_iota(jnp.int32, (length, length), 1)
    doc_column = doc_wide[:, :1]
    doc_row = jnp.sum(jnp.where(query_index == key_index, doc_column, 0.0), axis=0, keepdims=True)
    allowed = (key_index <= query_index) & (doc_row == doc_column)

    def sent_by(from_z):
        if from_z in (per_half - 1, per_half):
            return z != from_z
        return (z != from_z) & (z // per_half == from_z // per_half)

    for from_z in range(layers):
        @pl.when(sent_by(from_z))
        def _(from_z=from_z):
            for s in range(sp_count):
                arrive(parts.at[from_z, s * tokens:(s + 1) * tokens], part_sem.at[from_z, s])
    raw = parts[z] + parts[z + 1 - 2 * (z % 2)] + parts[per_half - z // per_half]
    raw_keys = raw[:, :HEAD_DIM]
    key_heads = (
        raw_keys * cosines[...] + pltpu.roll(raw_keys, HEAD_DIM // 2, 1) * sines[...]
    ).astype(jnp.bfloat16)
    value_heads = raw[:, HEAD_DIM:].astype(jnp.bfloat16)
    factor = HEAD_DIM ** (-0.5)
    my_seq, my_head = z // per_half, y * per_half + z % per_half
    group_size = head_cols // HEAD_DIM
    outs = (out0, out1)
    for g in range(group_size):
        columns = slice(g * HEAD_DIM, (g + 1) * HEAD_DIM)
        scores = lax.dot_general(
            query_rows[:, columns], key_heads, (((1,), (1,)), ((), ())), preferred_element_type=jnp.float32
        ) * factor
        scores = jnp.where(allowed, scores, MASKED)
        highest = jnp.max(scores, axis=-1, keepdims=True)
        exponent = jnp.where(allowed, jnp.exp(scores - highest), 0.0)
        weights = (exponent / jnp.sum(exponent, axis=-1, keepdims=True)).astype(jnp.bfloat16)
        mixed[g] = jnp.dot(weights, value_heads, preferred_element_type=jnp.float32).astype(jnp.bfloat16)
        head = my_head * group_size + g
        out_columns = pl.ds(pl.multiple_of(head * HEAD_DIM, 128), HEAD_DIM)
        for s in range(sp_count):
            own = (sp == s) & (core == my_seq)
            for m in range(2):
                src = mixed.at[g, s * tokens:(s + 1) * tokens]
                dst, recv = outs[m].at[0, :, out_columns], out_sem.at[m, head]
                put(src, dst, recv, {"sp": s, "fsdp": my_seq}, (core == m) & jnp.logical_not(own))

                @pl.when((core == m) & own)
                def _(src=src, dst=dst, recv=recv):
                    pltpu.make_async_copy(src, dst, recv).start()
    for m in range(2):
        for head in range(2 * per_half * group_size):
            arrive(outs[m].at[0, :, head * HEAD_DIM:(head + 1) * HEAD_DIM], out_sem.at[m, head])
    for away, make in pending:
        if away is None:
            make().wait_send()
        else:
            @pl.when(away)
            def _(make=make):
                make().wait_send()


def fused(mesh, hiddens, queries, documents, gains, keys, values):
    sp = mesh.shape["sp"]
    tokens, features = hiddens[0].shape[1], keys[0].shape[0]
    kv_heads = keys[0].shape[1] // HEAD_DIM
    head_cols = queries[0].shape[2] // kv_heads
    layers, length, half = sp // 2, sp * tokens, keys[0].shape[1] // 2
    half_dim = HEAD_DIM // 2
    frequency = ROPE_BASE ** (-2.0 * np.arange(half_dim) / HEAD_DIM)
    angles = np.arange(length)[:, None] * frequency[None, :]
    cosines = np.concatenate([np.cos(angles), np.cos(angles)], axis=1).astype(np.float32)
    sines = np.concatenate([-np.sin(angles), np.sin(angles)], axis=1).astype(np.float32)
    dma = pltpu.SemaphoreType.DMA
    bf16, f32 = jnp.bfloat16, jnp.float32
    sends = 2 * layers + 12 + 4 * layers + 4 * kv_heads + layers + sp * layers
    group_size = head_cols // HEAD_DIM
    sends = sends + 2 + 2 * group_size * sp + 2 * sp * layers
    return pl.pallas_call(
        functools.partial(fused_kernel, sp),
        out_shape=(jax.ShapeDtypeStruct((1, tokens, queries[0].shape[2]), bf16),) * 2,
        in_specs=[pl.BlockSpec(memory_space=pl.ANY)] * 8 + [pl.BlockSpec(memory_space=pltpu.VMEM)] * 6,
        out_specs=(pl.BlockSpec(memory_space=pltpu.VMEM),) * 2,
        scratch_shapes=[
            pltpu.VMEM((2,) + hiddens[0].shape[1:], bf16),
            dma((2,)),
            pltpu.VMEM((sp, 2 * tokens, 4 * features), bf16),
            pltpu.VMEM((4 * features, half), bf16),
            pltpu.VMEM((4 * features, half), bf16),
            pltpu.VMEM((2, 1, features), f32),
            pltpu.VMEM((2, 1, 128), f32),
            pltpu.VMEM((4, 1, features), f32),
            pltpu.VMEM((2, 1, 128), f32),
            pltpu.VMEM((2 * sp, 1, 128), f32),
            pltpu.VMEM((length, head_cols), bf16),
            pltpu.VMEM((sp, 1, 128), f32),
            pltpu.VMEM((sp * layers, tokens, 2 * HEAD_DIM), f32),
            pltpu.VMEM((sp * layers, tokens, 2 * HEAD_DIM), f32),
            pltpu.VMEM((layers, length, 2 * HEAD_DIM), f32),
            pltpu.VMEM((length, 128), f32),
            pltpu.VMEM((group_size, length, HEAD_DIM), bf16),
            dma((sends,)),
            dma((layers, 2)),
            dma((layers,)),
            dma((4, 2)),
            dma((4,)),
            dma((2 * sp,)),
            dma((sp,)),
            dma((sp,)),
            dma((layers, sp)),
            dma((sp * layers,)),
            dma((2, kv_heads * group_size)),
        ],
        compiler_params=pltpu.CompilerParams(collective_id=0, has_side_effects=True),
        name="fused",
    )(
        *hiddens, *queries, *keys, *values,
        *gains, *documents, cosines, sines,
    )


def per_device(
    mesh,
    policy_hidden,
    policy_queries,
    policy_documents,
    policy_gain,
    policy_key_weight,
    policy_value_weight,
    frozen_hidden,
    frozen_queries,
    frozen_documents,
    frozen_gain,
    frozen_key_weight,
    frozen_value_weight,
):
    if fits(mesh, policy_hidden, policy_queries, policy_key_weight):
        return fused(
            mesh,
            (policy_hidden, frozen_hidden),
            (policy_queries, frozen_queries),
            (policy_documents, frozen_documents),
            (policy_gain, frozen_gain),
            (policy_key_weight, frozen_key_weight),
            (policy_value_weight, frozen_value_weight),
        )
    policy_mixed = run_model(
        policy_hidden,
        policy_queries,
        policy_documents,
        policy_gain,
        policy_key_weight,
        policy_value_weight,
    )
    frozen_mixed = run_model(
        frozen_hidden,
        frozen_queries,
        frozen_documents,
        frozen_gain,
        frozen_key_weight,
        frozen_value_weight,
    )
    return (policy_mixed, frozen_mixed)


def solution(mesh):
    return jax.shard_map(
        functools.partial(per_device, mesh),
        mesh=mesh,
        in_specs=(
            P(("groups", "fsdp"), "sp", None),
            P(("groups", "fsdp"), "sp", None),
            P(("groups", "fsdp"), "sp"),
            P(("sp", "fsdp")),
            P(("sp", "fsdp"), None),
            P(("sp", "fsdp"), None),
            P(("groups", "fsdp"), "sp", None),
            P(("groups", "fsdp"), "sp", None),
            P(("groups", "fsdp"), "sp"),
            P(("sp", "fsdp")),
            P(("sp", "fsdp"), None),
            P(("sp", "fsdp"), None),
        ),
        out_specs=(P(("groups", "fsdp"), "sp", None), P(("groups", "fsdp"), "sp", None)),
        check_vma=False,
    )
```

profile of v0, /device:TPU:0, one launch (start us, length us, event | category | flops | bytes accessed | tf_op | source)
XLA Modules:
  0.0 56.0 jit_solution(8535611271527436598)
XLA Ops:
  0.6 53.2 %fused.1 = (bf16[1,32,1024]{2,1,0:T(8,128)(2,1)}, bf16[1,32,1024]{2,1,0:T(8,128)(2,1)}) custom-call(bf16[1,32,4096]{2,1,0:T(8,128)(2,1)} %hidden0.1, bf16[1,32,4096]{2,1,0:T(8,128)(2,1)} %hidden1.1, bf16[1,32,1024]{2,1,0:T(8,128)(2,1)} %queries0.1, bf16[1,32,1024]{2,1,0:T(8,128)(2,1)} %queries1.1, bf16[256,512]{1,0:T(8,128)(2,1)} %key0.1, ...), custom_call_target="tpu_custom_call" | custom-call | tf_op jit(solution)/shard_map/fused/pallas_call | solution.py:431
  53.9 0.0 copy-start
  53.9 1.5 %copy.18 = bf16[1,32,1024]{2,1,0:T(8,128)(2,1)} copy(bf16[1,32,1024]{2,1,0:T(8,128)(2,1)} %get-tuple-element.4) | data formatting | bytes 131072
  55.4 0.0 copy-done
  55.4 0.6 %copy.19 = bf16[1,32,1024]{2,1,0:T(8,128)(2,1)} copy(bf16[1,32,1024]{2,1,0:T(8,128)(2,1)S(1)} %copy-done) | data formatting | bytes 131072
Async XLA Ops:
  53.9 1.5 %copy-start = (bf16[1,32,1024]{2,1,0:T(8,128)(2,1)S(1)}, bf16[1,32,1024]{2,1,0:T(8,128)(2,1)}, u32[]{:S(2)}) copy-start(bf16[1,32,1024]{2,1,0:T(8,128)(2,1)} %get-tuple-element.5) | copy-start | bytes 196612
where the time goes:
time: 56.2 us; the launch traced here: 56 us
  Pallas kernels  53.2 us (95%)
  local copies, waits for them, and re-layouts  2.14 us (4%)
  between operations  0.65 us (1%)
    pallas_call x1, Pallas kernels, fused(): pl.pallas_call(functools.partial(fused_kernel, sp), out_shape=(jax.ShapeD...  53.2 us
    unnamed x4, local copies, waits for them, and re-layouts  2.14 us

commit v1 on v0

v1 whole, which is shorter than its diff:
```python
import contextlib
import functools

import jax
import jax.numpy as jnp
import numpy as np
from jax import lax
from jax.experimental import pallas as pl
from jax.experimental.pallas import tpu as pltpu
from jax.sharding import PartitionSpec as P

HEAD_DIM = 128


EPS = 1e-05
ROPE_BASE = 500000.0
MASKED = -1e30


def rotate(raw_keys, positions):
    half_dim = HEAD_DIM // 2
    frequency = jnp.exp(
        -jnp.log(ROPE_BASE) * jnp.arange(half_dim, dtype=jnp.float32) * 2.0 / HEAD_DIM
    )
    angles = positions.astype(jnp.float32)[:, None] * frequency[None, :]
    cosines = jnp.cos(angles)[:, None, :]
    sines = jnp.sin(angles)[:, None, :]
    front_half = raw_keys[..., :half_dim]
    back_half = raw_keys[..., half_dim:]
    return jnp.concatenate(
        [front_half * cosines - back_half * sines, back_half * cosines + front_half * sines],
        axis=-1,
    )


def project(hidden, gain, key_weight, value_weight):
    tokens = hidden.shape[1]
    widened = hidden[0].astype(jnp.float32)
    inverse = lax.rsqrt(jnp.mean(widened * widened, axis=-1, keepdims=True) + EPS)
    scaled = widened * inverse
    gain_rows = lax.all_gather(gain, ("sp", "fsdp"), axis=0, tiled=True)
    key_rows = lax.all_gather(key_weight, ("sp", "fsdp"), axis=0, tiled=True)
    value_rows = lax.all_gather(value_weight, ("sp", "fsdp"), axis=0, tiled=True)
    normed = (scaled * gain_rows.astype(jnp.float32)[None, :]).astype(jnp.bfloat16)
    raw_keys = jnp.dot(normed, key_rows, preferred_element_type=jnp.float32)
    raw_values = jnp.dot(normed, value_rows, preferred_element_type=jnp.float32)
    positions = lax.axis_index("sp") * tokens + jnp.arange(tokens, dtype=jnp.int32)
    key_heads = rotate(raw_keys.reshape(tokens, -1, HEAD_DIM), positions).astype(jnp.bfloat16)
    value_heads = raw_values.astype(jnp.bfloat16).reshape(tokens, -1, HEAD_DIM)
    return (key_heads, value_heads)


def attend(queries, key_heads, value_heads, documents):
    length = queries.shape[0]
    head_count = queries.shape[1]
    block_rows = min(512, length)
    margin = min(512, length // 2)
    window = block_rows + margin
    factor = HEAD_DIM ** (-0.5)
    offsets = jnp.arange(block_rows, dtype=jnp.int32)
    window_offsets = jnp.arange(window, dtype=jnp.int32)
    padding = jnp.zeros((margin, head_count, HEAD_DIM), jnp.bfloat16)
    padded_keys = jnp.concatenate([padding, key_heads], axis=0)
    padded_values = jnp.concatenate([padding, value_heads], axis=0)
    padded_docs = jnp.concatenate([jnp.full((margin,), -1, jnp.int32), documents], axis=0)

    def one_block(block_index):
        first = block_index * block_rows
        query_block = lax.dynamic_slice_in_dim(queries, first, block_rows, 0)
        query_docs = lax.dynamic_slice_in_dim(documents, first, block_rows, 0)
        query_positions = first + offsets
        key_block = lax.dynamic_slice_in_dim(padded_keys, first, window, 0)
        value_block = lax.dynamic_slice_in_dim(padded_values, first, window, 0)
        key_docs = lax.dynamic_slice_in_dim(padded_docs, first, window, 0)
        key_positions = first - margin + window_offsets
        allowed = (key_positions[None, :] <= query_positions[:, None]) & (
            key_docs[None, :] == query_docs[:, None]
        )
        scores = (
            jnp.einsum("qnd,knd->nqk", query_block, key_block, preferred_element_type=jnp.float32)
            * factor
        )
        scores = jnp.where(allowed[None], scores, MASKED)
        highest = jnp.max(scores, axis=-1, keepdims=True)
        exponent = jnp.where(allowed[None], jnp.exp(scores - highest), 0.0)
        weights = (exponent / jnp.sum(exponent, axis=-1, keepdims=True)).astype(jnp.bfloat16)
        blended = jnp.einsum(
            "nqk,knd->qnd", weights, value_block, preferred_element_type=jnp.float32
        )
        return blended.astype(jnp.bfloat16)

    blocks = lax.map(one_block, jnp.arange(length // block_rows, dtype=jnp.int32))
    return blocks.reshape(length, head_count, HEAD_DIM)


def run_model(hidden, queries, documents, gain, key_weight, value_weight):
    tokens = hidden.shape[1]
    head_count = queries.shape[2] // HEAD_DIM
    query_local = queries[0].reshape(tokens, head_count, HEAD_DIM)
    every_doc = lax.all_gather(documents[0], "sp", axis=0, tiled=True)
    key_heads, value_heads = project(hidden, gain, key_weight, value_weight)
    group_size = head_count // key_heads.shape[1]
    wide_keys = jnp.repeat(key_heads, group_size, axis=1)
    wide_values = jnp.repeat(value_heads, group_size, axis=1)
    query_spread, key_spread, value_spread = (
        lax.all_to_all(query_local, "sp", split_axis=1, concat_axis=0, tiled=True),
        lax.all_to_all(wide_keys, "sp", split_axis=1, concat_axis=0, tiled=True),
        lax.all_to_all(wide_values, "sp", split_axis=1, concat_axis=0, tiled=True),
    )
    mixed = attend(query_spread, key_spread, value_spread, every_doc)
    returned = lax.all_to_all(mixed, "sp", split_axis=0, concat_axis=1, tiled=True)
    return returned.reshape(1, tokens, head_count * HEAD_DIM)


MESH = pl.DeviceIdType.MESH
TRACE = False


def fits(mesh, hidden, queries, key_weight):
    sp, cores = mesh.shape["sp"], mesh.shape["fsdp"]
    tokens = hidden.shape[1]
    kv_heads = key_weight.shape[1] // HEAD_DIM
    return (
        cores == 2
        and mesh.shape["groups"] == 2
        and sp == 8
        and kv_heads == 4
        and queries.shape[2] % (kv_heads * HEAD_DIM) == 0
        and key_weight.shape[0] % 128 == 0
        and hidden.shape[2] == key_weight.shape[0] * sp * cores
        and tokens % 16 == 0
        and tokens <= 64
    )


def fused_kernel(
    hidden0, hidden1, queries0, queries1, key0, key1, value0, value1, cosine_table, sine_table,
    gain0, gain1, documents0, documents1,
    out,
    gain_raw0, gain_raw1, doc_raw, near, rows, wide, normed, gain_send, gain_rows, row_send, row_data, query_rows, doc_wide,
    key_send, value_send, key_parts, value_parts, home, key_heads, value_heads, mixed, cosines, sines,
    raw_sem, near_sem, table_sem, send_sem, row_sem, wide_sem, gain_sem, data_sem, query_sem, part_sem, value_sem, out_sem,
):
    hiddens, queries = (hidden0, hidden1), (queries0, queries1)
    keys, values = (key0, key1), (value0, value1)
    tokens, features = hidden0.shape[1], key0.shape[0]
    slab = 8 * features
    head_cols = query_rows.shape[1]
    group_size = head_cols // HEAD_DIM
    length = query_rows.shape[0]
    sp, core, plane = lax.axis_index("sp"), lax.axis_index("fsdp"), lax.axis_index("groups")
    z, y = sp // 2, sp % 2
    upper, parity = z // 2, z % 2
    near_z = z + 1 - 2 * parity
    far_z = lax.rem(z + 2, 4)
    me = (plane * 8 + sp) * 2 + core

    barrier = pltpu.get_barrier_semaphore()
    for step in range(1, 32):
        other = lax.rem(me + step, 32)
        pl.semaphore_signal(
            barrier, inc=1, device_id={"groups": other // 16, "sp": (other // 2) % 8, "fsdp": other % 2},
            device_id_type=MESH,
        )

    def scope(name):
        return jax.named_scope(name) if TRACE else contextlib.nullcontext()

    def place(zz, yy, cc):
        return (zz * 2 + yy) * 2 + cc

    def place_rows(index):
        return pl.ds(pl.multiple_of(index * features, 128), features)

    mine = place(parity, y, core)

    def columns(half, b):
        return pl.ds(pl.multiple_of((half * 2 + b) * HEAD_DIM, HEAD_DIM), HEAD_DIM)

    for m in range(2):
        pltpu.make_async_copy(hiddens[m].at[0], near.at[m], near_sem.at[m]).start()

        @pl.when(plane == m)
        def _(m=m):
            for b in range(2):
                target = wide.at[b, place_rows(mine)]
                pltpu.make_async_copy(
                    keys[m].at[:, columns(y, b)], target.at[:, :HEAD_DIM], wide_sem.at[b, mine]
                ).start()
                pltpu.make_async_copy(
                    values[m].at[:, columns(y, b)], target.at[:, HEAD_DIM:], wide_sem.at[b, mine]
                ).start()

    small = (
        (gain0, gain_raw0), (gain1, gain_raw1), (documents0, doc_raw.at[0]), (documents1, doc_raw.at[1]),
    )
    for index, (src, dst) in enumerate(small):
        pltpu.make_async_copy(src, dst, raw_sem.at[index]).start()
    pltpu.make_async_copy(cosine_table, cosines, table_sem.at[0]).start()
    pltpu.make_async_copy(sine_table, sines, table_sem.at[1]).start()
    with scope("wbar"):
        pl.semaphore_wait(barrier, 31)

    pending = []

    def put(src, dst, recv, target, away=None):
        slot = len(pending)

        def make():
            return pltpu.make_async_remote_copy(
                src_ref=src, dst_ref=dst, send_sem=send_sem.at[slot], recv_sem=recv,
                device_id=target, device_id_type=MESH,
            )

        pending.append((away, make))
        if away is None:
            make().start()
        else:
            @pl.when(away)
            def _():
                make().start()

    def send(src, dst, recv, target, own):
        put(src, dst, recv, target, jnp.logical_not(own))

        @pl.when(own)
        def _():
            pltpu.make_async_copy(src, dst, recv).start()

    def put_weight(b, half, target):
        slot = len(pending)
        for index, weights in enumerate((keys, values)):
            cols = slice(index * HEAD_DIM, (index + 1) * HEAD_DIM)

            def make(m, index=index, weights=weights, cols=cols):
                return pltpu.make_async_remote_copy(
                    src_ref=weights[m].at[:, columns(half, b)], dst_ref=wide.at[b, place_rows(mine), cols],
                    send_sem=send_sem.at[slot + index], recv_sem=wide_sem.at[b, mine],
                    device_id=target, device_id_type=MESH,
                )

            for m in range(2):
                @pl.when(plane == m)
                def _(m=m, make=make):
                    make(m).start()
            pending.append((None, functools.partial(make, 0)))

    def arrive(dst, recv, name):
        with scope(name):
            pltpu.make_async_copy(dst, dst, recv).wait()

    def forward(b, index, targets):
        block = wide.at[b, place_rows(index)]
        for target in targets:
            put(block, block, wide_sem.at[b, index], target)

    def arrive_weight(b, index, name):
        block = wide.at[b, place_rows(index)]
        arrive(block, wide_sem.at[b, index], name)

    across, beside, along = {"sp": z * 2 + 1 - y}, {"fsdp": 1 - core}, {"sp": near_z * 2 + y}
    beyond = {"sp": near_z * 2 + 1 - y}
    away_head, home_head = 1 - upper, upper

    put_weight(away_head, 1 - y, across)
    put_weight(away_head, y, along)
    put_weight(away_head, 1 - y, beyond)
    put_weight(away_head, y, beside)
    put_weight(home_head, 1 - y, across)
    for m in range(2):
        pltpu.make_async_copy(hiddens[m].at[0], near.at[m], near_sem.at[m]).wait()

    def put_hidden(h):
        to_z = 2 * h + core
        for other in range(2):
            m = plane if other == 0 else 1 - plane
            src, dst = near.at[m, :, pl.ds(pl.multiple_of(h * slab, 128), slab)], rows.at[sp]
            target = {"groups": m, "sp": to_z * 2 + y, "fsdp": plane}
            if other:
                put(src, dst, row_sem.at[sp], target)
            else:
                send(src, dst, row_sem.at[sp], target, (to_z == z) & (core == plane))

    for index, (src, dst) in enumerate(small):
        pltpu.make_async_copy(src, dst, raw_sem.at[index]).wait()
    gain_send[...] = jnp.where(
        plane == 0, gain_raw0[...].astype(jnp.float32), gain_raw1[...].astype(jnp.float32)
    ).reshape(1, -1)
    for zz in range(2):
        for yy in range(2):
            for cc in range(2):
                own = (parity == zz) & (y == yy) & (core == cc)
                send(
                    gain_send, gain_rows.at[mine], gain_sem,
                    {"sp": (upper * 2 + zz) * 2 + yy, "fsdp": cc}, own,
                )
    square = (
        lax.broadcasted_iota(jnp.int32, (tokens, 128), 0)
        == lax.broadcasted_iota(jnp.int32, (tokens, 128), 1)
    )
    for m in range(2):
        wide_row = near[m].astype(jnp.float32)
        inverse = lax.rsqrt(jnp.mean(wide_row * wide_row, axis=-1, keepdims=True) + EPS)
        row_send[m] = jnp.zeros((8, 128), jnp.float32)
        row_send[m, 0:1, :] = jnp.sum(jnp.where(square, inverse, 0.0), axis=0, keepdims=True)
        row_send[m, 1:2, :tokens] = doc_raw[m].astype(jnp.float32)
    for m in range(2):
        for yy in range(2):
            for h in range(2):
                to_z = 2 * h + core
                send(
                    row_send.at[m], row_data.at[sp], data_sem,
                    {"groups": m, "sp": to_z * 2 + yy, "fsdp": plane},
                    (plane == m) & (y == yy) & (to_z == z) & (core == plane),
                )
    put_hidden(upper)
    put_hidden(1 - upper)
    put_weight(home_head, y, along)
    put_weight(home_head, y, beside)

    place_y, place_z, place_zy = place(parity, 1 - y, core), place(1 - parity, y, core), place(1 - parity, 1 - y, core)

    def pass_rows(step):
        from_z = order[step]
        block = from_z * 2 + y
        arrive(rows.at[block], row_sem.at[block], f"whid{step}")
        put(rows.at[block], rows.at[block], row_sem.at[block], across)

    order = (z, near_z + upper * (1 - near_z), 2 * (1 - upper), 3 + upper * (near_z - 3))
    pass_rows(0)
    arrive_weight(away_head, place_y, "wy0")
    forward(away_head, place_y, (beside,))
    arrive_weight(away_head, place_z, "wz0")
    forward(away_head, place_z, (beside,))
    arrive_weight(away_head, place_zy, "wzy0")
    forward(away_head, place_zy, (beside,))
    arrive_weight(home_head, place_y, "wy1")
    forward(home_head, place_y, (along, beside))
    pass_rows(1)
    arrive(gain_rows, gain_sem, "wgain")
    arrive(row_data, data_sem, "wdata")
    arrive_weight(away_head, mine, "wown0")
    for zz in range(2):
        for yy in range(2):
            arrive_weight(away_head, place(zz, yy, 1 - core), "wside0")
    gain_row = jnp.concatenate([gain_rows[s] for s in range(8)], axis=1)
    partner = {"sp": far_z * 2 + y}

    def block_of(index, k):
        return index // 2 * 4 + 2 * k + (y if index % 2 == 0 else 1 - y)

    def project(index):
        for k in range(2):
            s = block_of(index, k)
            scale = jnp.sum(jnp.where(square, row_data[s, 0:1, :], 0.0), axis=1, keepdims=True)
            normed[index, k * tokens:(k + 1) * tokens, :] = (
                rows[s].astype(jnp.float32) * scale * gain_row
            ).astype(jnp.bfloat16)
        part = jnp.dot(normed[index], wide[away_head], preferred_element_type=jnp.float32)
        key_send[index] = part[:, :HEAD_DIM]
        value_send[index] = part[:, HEAD_DIM:].astype(jnp.bfloat16)
        put(key_send.at[index], key_parts.at[index], part_sem.at[index], partner)
        put(value_send.at[index], value_parts.at[index], value_sem.at[index], partner)

    def arrive_rows(index):
        for k in range(2):
            block = block_of(index, k)
            arrive(rows.at[block], row_sem.at[block], f"wfwd{index}")

    pass_rows(2)
    project(0)
    pass_rows(3)
    arrive_rows(1)
    project(1)
    token_rows = pl.ds(pl.multiple_of(sp * tokens, 16), tokens)
    for m in range(2):
        for yy in range(2):
            for h in range(2):
                to_z, head = 2 * h + core, yy * 2 + h
                send(
                    queries[m].at[0, :, head * head_cols:(head + 1) * head_cols],
                    query_rows.at[token_rows], query_sem.at[upper],
                    {"groups": m, "sp": to_z * 2 + yy, "fsdp": plane},
                    (plane == m) & (y == yy) & (to_z == z) & (core == plane),
                )

    project(2)
    arrive_weight(home_head, place_z, "wz1")
    forward(home_head, place_z, (beside,))
    arrive_rows(3)
    project(3)

    for s in range(8):
        column = jnp.sum(jnp.where(square, row_data[s, 1:2, :], 0.0), axis=1, keepdims=True)
        doc_wide[s * tokens:(s + 1) * tokens, :] = jnp.broadcast_to(column, (tokens, 128))
    query_index = lax.broadcasted_iota(jnp.int32, (length, length), 0)
    key_index = lax.broadcasted_iota(jnp.int32, (length, length), 1)
    doc_column = doc_wide[:, :1]
    doc_row = jnp.sum(jnp.where(query_index == key_index, doc_column, 0.0), axis=0, keepdims=True)
    arrive_weight(home_head, place_zy, "wzy1")
    forward(home_head, place_zy, (beside,))
    for index in range(2):
        pltpu.make_async_copy((cosine_table, sine_table)[index], (cosines, sines)[index], table_sem.at[index]).wait()
    arrive_weight(home_head, mine, "wown1")
    for zz in range(2):
        for yy in range(2):
            arrive_weight(home_head, place(zz, yy, 1 - core), "wside1")

    for index in range(4):
        own_part = jnp.dot(normed[index], wide[home_head], preferred_element_type=jnp.float32)
        for k in range(2):
            block = pl.ds(pl.multiple_of(block_of(index, k) * tokens, 16), tokens)
            home[block, :] = own_part[k * tokens:(k + 1) * tokens, :]
    factor = HEAD_DIM ** (-0.5)
    head = y * 2 + upper
    out_columns = pl.ds(pl.multiple_of(head * head_cols, 128), head_cols)
    half_rows = length // 2
    for half in range(2):
        for index in range(2 * half, 2 * half + 2):
            arrive(key_parts.at[index], part_sem.at[index], f"wpart{index}")
            arrive(value_parts.at[index], value_sem.at[index], f"wpart{index}")
            for k in range(2):
                block = pl.ds(pl.multiple_of(block_of(index, k) * tokens, 16), tokens)
                near_rows = slice(k * tokens, (k + 1) * tokens)
                raw_keys = home[block, :HEAD_DIM] + key_parts[index, near_rows, :]
                raw_values = home[block, HEAD_DIM:] + value_parts[index, near_rows, :].astype(jnp.float32)
                key_heads[block, :] = (
                    raw_keys * cosines[block, :] + pltpu.roll(raw_keys, HEAD_DIM // 2, 1) * sines[block, :]
                ).astype(jnp.bfloat16)
                value_heads[block, :] = raw_values.astype(jnp.bfloat16)
        first, last = half * half_rows, (half + 1) * half_rows
        arrive(query_rows.at[first:last], query_sem.at[half], f"wq{half}")
        allowed = (
            lax.broadcasted_iota(jnp.int32, (half_rows, last), 1)
            <= first + lax.broadcasted_iota(jnp.int32, (half_rows, last), 0)
        ) & (doc_row[:, :last] == doc_wide[first:last, :1])
        for g in range(group_size):
            cols = slice(g * HEAD_DIM, (g + 1) * HEAD_DIM)
            scores = lax.dot_general(
                query_rows[first:last, cols], key_heads[:last, :], (((1,), (1,)), ((), ())),
                preferred_element_type=jnp.float32,
            ) * factor
            scores = jnp.where(allowed, scores, MASKED)
            highest = jnp.max(scores, axis=-1, keepdims=True)
            exponent = jnp.where(allowed, jnp.exp(scores - highest), 0.0)
            weights = (exponent / jnp.sum(exponent, axis=-1, keepdims=True)).astype(jnp.bfloat16)
            mixed[half, :, cols] = jnp.dot(
                weights, value_heads[:last, :], preferred_element_type=jnp.float32
            ).astype(jnp.bfloat16)
        for k in range(4):
            to_sp = half * 4 + k
            send(
                mixed.at[half, k * tokens:(k + 1) * tokens], out.at[plane, 0, :, out_columns], out_sem,
                {"groups": core, "sp": to_sp, "fsdp": parity},
                (core == plane) & (sp == to_sp) & (core == parity),
            )
    with scope("wsend"):
        for away, make in pending:
            if away is None:
                make().wait_send()
            else:
                @pl.when(away)
                def _(make=make):
                    make().wait_send()
    arrive(out, out_sem, "wout")


def fused(mesh, hiddens, queries, documents, gains, keys, values):
    sp = mesh.shape["sp"]
    tokens, features = hiddens[0].shape[1], keys[0].shape[0]
    kv_heads = keys[0].shape[1] // HEAD_DIM
    head_cols = queries[0].shape[2] // kv_heads
    length = sp * tokens
    half_dim = HEAD_DIM // 2
    frequency = ROPE_BASE ** (-2.0 * np.arange(half_dim) / HEAD_DIM)
    angles = np.arange(length)[:, None] * frequency[None, :]
    cosines = np.concatenate([np.cos(angles), np.cos(angles)], axis=1).astype(np.float32)
    sines = np.concatenate([-np.sin(angles), np.sin(angles)], axis=1).astype(np.float32)
    dma = pltpu.SemaphoreType.DMA
    bf16, f32 = jnp.bfloat16, jnp.float32
    sends = 14 + 4 + 8 + 8 + 8 + 4 + 8 + 8 + 8
    out = pl.pallas_call(
        fused_kernel,
        out_shape=pltpu.VMEM((2, 1, tokens, queries[0].shape[2]), bf16),
        in_specs=[pl.BlockSpec(memory_space=pl.ANY)] * 14,
        out_specs=pl.BlockSpec(memory_space=pltpu.VMEM),
        scratch_shapes=[
            pltpu.VMEM((features,), bf16),
            pltpu.VMEM((features,), bf16),
            pltpu.VMEM((2, 1, tokens), jnp.int32),
            pltpu.VMEM((2,) + hiddens[0].shape[1:], bf16),
            pltpu.VMEM((sp, tokens, 8 * features), bf16),
            pltpu.VMEM((2, 8 * features, 2 * HEAD_DIM), bf16),
            pltpu.VMEM((4, 2 * tokens, 8 * features), bf16),
            pltpu.VMEM((1, features), f32),
            pltpu.VMEM((8, 1, features), f32),
            pltpu.VMEM((2, 8, 128), f32),
            pltpu.VMEM((sp, 8, 128), f32),
            pltpu.VMEM((length, head_cols), bf16),
            pltpu.VMEM((length, 128), f32),
            pltpu.VMEM((4, 2 * tokens, HEAD_DIM), f32),
            pltpu.VMEM((4, 2 * tokens, HEAD_DIM), bf16),
            pltpu.VMEM((4, 2 * tokens, HEAD_DIM), f32),
            pltpu.VMEM((4, 2 * tokens, HEAD_DIM), bf16),
            pltpu.VMEM((length, 2 * HEAD_DIM), f32),
            pltpu.VMEM((length, HEAD_DIM), bf16),
            pltpu.VMEM((length, HEAD_DIM), bf16),
            pltpu.VMEM((2, length // 2, head_cols), bf16),
            pltpu.VMEM((length, HEAD_DIM), f32),
            pltpu.VMEM((length, HEAD_DIM), f32),
            dma((4,)),
            dma((2,)),
            dma((2,)),
            dma((sends,)),
            dma((sp,)),
            dma((2, 8)),
            dma(()),
            dma(()),
            dma((2,)),
            dma((4,)),
            dma((4,)),
            dma(()),
        ],
        compiler_params=pltpu.CompilerParams(collective_id=0, has_side_effects=True),
        name="fused",
    )(
        *hiddens, *queries, *keys, *values, cosines, sines,
        *gains, *documents,
    )
    return out[0], out[1]


def per_device(
    mesh,
    policy_hidden,
    policy_queries,
    policy_documents,
    policy_gain,
    policy_key_weight,
    policy_value_weight,
    frozen_hidden,
    frozen_queries,
    frozen_documents,
    frozen_gain,
    frozen_key_weight,
    frozen_value_weight,
):
    if fits(mesh, policy_hidden, policy_queries, policy_key_weight):
        return fused(
            mesh,
            (policy_hidden, frozen_hidden),
            (policy_queries, frozen_queries),
            (policy_documents, frozen_documents),
            (policy_gain, frozen_gain),
            (policy_key_weight, frozen_key_weight),
            (policy_value_weight, frozen_value_weight),
        )
    policy_mixed = run_model(
        policy_hidden,
        policy_queries,
        policy_documents,
        policy_gain,
        policy_key_weight,
        policy_value_weight,
    )
    frozen_mixed = run_model(
        frozen_hidden,
        frozen_queries,
        frozen_documents,
        frozen_gain,
        frozen_key_weight,
        frozen_value_weight,
    )
    return (policy_mixed, frozen_mixed)


def solution(mesh):
    return jax.shard_map(
        functools.partial(per_device, mesh),
        mesh=mesh,
        in_specs=(
            P(("groups", "fsdp"), "sp", None),
            P(("groups", "fsdp"), "sp", None),
            P(("groups", "fsdp"), "sp"),
            P(("sp", "fsdp")),
            P(("sp", "fsdp"), None),
            P(("sp", "fsdp"), None),
            P(("groups", "fsdp"), "sp", None),
            P(("groups", "fsdp"), "sp", None),
            P(("groups", "fsdp"), "sp"),
            P(("sp", "fsdp")),
            P(("sp", "fsdp"), None),
            P(("sp", "fsdp"), None),
        ),
        out_specs=(P(("groups", "fsdp"), "sp", None), P(("groups", "fsdp"), "sp", None)),
        check_vma=False,
    )
```

time: 56.2 us -> 44.7 us (0.80)
  Pallas kernels: 53.2 us -> 42.8 us
  local copies, waits for them, and re-layouts: 2.14 us -> 0.66 us
    pallas_call x1, Pallas kernels: 53.2 us -> 42.8 us  [fused(): pl.pallas_call(fused_kernel, out_shape=pltpu.VMEM((2, 1, tokens, queries[...]
    unnamed x4 -> x0, local copies, waits for them, and re-layouts: 2.14 us -> none
    squeeze x0 -> x1, local copies, waits for them, and re-layouts: none -> 0.66 us  [fused(): return (out[0], out[1])]
where the time goes in v1:
time: 44.7 us; the launch traced here: 44.1 us
  Pallas kernels  42.8 us (96%)
  local copies, waits for them, and re-layouts  0.66 us (1%)
  between operations  0.64 us (1%)
    pallas_call x1, Pallas kernels, fused(): pl.pallas_call(fused_kernel, out_shape=pltpu.VMEM((2, 1, tokens, queries[...  42.8 us

profile of v1, /device:TPU:0, one launch (start us, length us, event | category | flops | bytes accessed | tf_op | source)
XLA Modules:
  0.0 44.1 jit_solution(4907441040146883869)
XLA Ops:
  0.6 42.8 %fused.1 = bf16[2,1,32,1024]{3,2,1,0:T(8,128)(2,1)S(1)} custom-call(bf16[1,32,4096]{2,1,0:T(8,128)(2,1)} %hidden0.1, bf16[1,32,4096]{2,1,0:T(8,128)(2,1)} %hidden1.1, bf16[1,32,1024]{2,1,0:T(8,128)(2,1)} %queries0.1, bf16[1,32,1024]{2,1,0:T(8,128)(2,1)} %queries1.1, bf16[256,512]{1,0:T(8,128)(2,1)} %key0.1, bf16[256,512]{1,0:T(8,128)(2,1)} %key1.1, ...), custom_call_target="tpu_custom_call" | custom-call | tf_op jit(solution)/shard_map/fused/pallas_call | solution.py:482
  43.4 0.7 %slice_bitcast_fusion = (bf16[1,32,1024]{2,1,0:T(8,128)(2,1)}, bf16[1,32,1024]{2,1,0:T(8,128)(2,1)}) fusion(bf16[2,1,32,1024]{3,2,1,0:T(8,128)(2,1)S(1)} %fused.1), kind=kLoop, calls=%fused_computation | loop fusion | bytes 262144 | tf_op jit(solution)/shard_map/squeeze | solution.py:530

commit v2 on v1

v2 whole, which is shorter than its diff:
```python
import contextlib
import functools

import jax
import jax.numpy as jnp
import numpy as np
from jax import lax
from jax.experimental import pallas as pl
from jax.experimental.pallas import tpu as pltpu
from jax.sharding import PartitionSpec as P

HEAD_DIM = 128


EPS = 1e-05
ROPE_BASE = 500000.0
MASKED = -1e30


def rotate(raw_keys, positions):
    half_dim = HEAD_DIM // 2
    frequency = jnp.exp(
        -jnp.log(ROPE_BASE) * jnp.arange(half_dim, dtype=jnp.float32) * 2.0 / HEAD_DIM
    )
    angles = positions.astype(jnp.float32)[:, None] * frequency[None, :]
    cosines = jnp.cos(angles)[:, None, :]
    sines = jnp.sin(angles)[:, None, :]
    front_half = raw_keys[..., :half_dim]
    back_half = raw_keys[..., half_dim:]
    return jnp.concatenate(
        [front_half * cosines - back_half * sines, back_half * cosines + front_half * sines],
        axis=-1,
    )


def project(hidden, gain, key_weight, value_weight):
    tokens = hidden.shape[1]
    widened = hidden[0].astype(jnp.float32)
    inverse = lax.rsqrt(jnp.mean(widened * widened, axis=-1, keepdims=True) + EPS)
    scaled = widened * inverse
    gain_rows = lax.all_gather(gain, ("sp", "fsdp"), axis=0, tiled=True)
    key_rows = lax.all_gather(key_weight, ("sp", "fsdp"), axis=0, tiled=True)
    value_rows = lax.all_gather(value_weight, ("sp", "fsdp"), axis=0, tiled=True)
    normed = (scaled * gain_rows.astype(jnp.float32)[None, :]).astype(jnp.bfloat16)
    raw_keys = jnp.dot(normed, key_rows, preferred_element_type=jnp.float32)
    raw_values = jnp.dot(normed, value_rows, preferred_element_type=jnp.float32)
    positions = lax.axis_index("sp") * tokens + jnp.arange(tokens, dtype=jnp.int32)
    key_heads = rotate(raw_keys.reshape(tokens, -1, HEAD_DIM), positions).astype(jnp.bfloat16)
    value_heads = raw_values.astype(jnp.bfloat16).reshape(tokens, -1, HEAD_DIM)
    return (key_heads, value_heads)


def attend(queries, key_heads, value_heads, documents):
    length = queries.shape[0]
    head_count = queries.shape[1]
    block_rows = min(512, length)
    margin = min(512, length // 2)
    window = block_rows + margin
    factor = HEAD_DIM ** (-0.5)
    offsets = jnp.arange(block_rows, dtype=jnp.int32)
    window_offsets = jnp.arange(window, dtype=jnp.int32)
    padding = jnp.zeros((margin, head_count, HEAD_DIM), jnp.bfloat16)
    padded_keys = jnp.concatenate([padding, key_heads], axis=0)
    padded_values = jnp.concatenate([padding, value_heads], axis=0)
    padded_docs = jnp.concatenate([jnp.full((margin,), -1, jnp.int32), documents], axis=0)

    def one_block(block_index):
        first = block_index * block_rows
        query_block = lax.dynamic_slice_in_dim(queries, first, block_rows, 0)
        query_docs = lax.dynamic_slice_in_dim(documents, first, block_rows, 0)
        query_positions = first + offsets
        key_block = lax.dynamic_slice_in_dim(padded_keys, first, window, 0)
        value_block = lax.dynamic_slice_in_dim(padded_values, first, window, 0)
        key_docs = lax.dynamic_slice_in_dim(padded_docs, first, window, 0)
        key_positions = first - margin + window_offsets
        allowed = (key_positions[None, :] <= query_positions[:, None]) & (
            key_docs[None, :] == query_docs[:, None]
        )
        scores = (
            jnp.einsum("qnd,knd->nqk", query_block, key_block, preferred_element_type=jnp.float32)
            * factor
        )
        scores = jnp.where(allowed[None], scores, MASKED)
        highest = jnp.max(scores, axis=-1, keepdims=True)
        exponent = jnp.where(allowed[None], jnp.exp(scores - highest), 0.0)
        weights = (exponent / jnp.sum(exponent, axis=-1, keepdims=True)).astype(jnp.bfloat16)
        blended = jnp.einsum(
            "nqk,knd->qnd", weights, value_block, preferred_element_type=jnp.float32
        )
        return blended.astype(jnp.bfloat16)

    blocks = lax.map(one_block, jnp.arange(length // block_rows, dtype=jnp.int32))
    return blocks.reshape(length, head_count, HEAD_DIM)


def run_model(hidden, queries, documents, gain, key_weight, value_weight):
    tokens = hidden.shape[1]
    head_count = queries.shape[2] // HEAD_DIM
    query_local = queries[0].reshape(tokens, head_count, HEAD_DIM)
    every_doc = lax.all_gather(documents[0], "sp", axis=0, tiled=True)
    key_heads, value_heads = project(hidden, gain, key_weight, value_weight)
    group_size = head_count // key_heads.shape[1]
    wide_keys = jnp.repeat(key_heads, group_size, axis=1)
    wide_values = jnp.repeat(value_heads, group_size, axis=1)
    query_spread, key_spread, value_spread = (
        lax.all_to_all(query_local, "sp", split_axis=1, concat_axis=0, tiled=True),
        lax.all_to_all(wide_keys, "sp", split_axis=1, concat_axis=0, tiled=True),
        lax.all_to_all(wide_values, "sp", split_axis=1, concat_axis=0, tiled=True),
    )
    mixed = attend(query_spread, key_spread, value_spread, every_doc)
    returned = lax.all_to_all(mixed, "sp", split_axis=0, concat_axis=1, tiled=True)
    return returned.reshape(1, tokens, head_count * HEAD_DIM)


MESH = pl.DeviceIdType.MESH
TRACE = False


def fits(mesh, hidden, queries, key_weight):
    sp, cores = mesh.shape["sp"], mesh.shape["fsdp"]
    tokens = hidden.shape[1]
    kv_heads = key_weight.shape[1] // HEAD_DIM
    return (
        cores == 2
        and mesh.shape["groups"] == 2
        and sp == 8
        and kv_heads == 4
        and queries.shape[2] % (kv_heads * HEAD_DIM) == 0
        and key_weight.shape[0] % 128 == 0
        and hidden.shape[2] == key_weight.shape[0] * sp * cores
        and tokens % 16 == 0
        and tokens <= 64
    )


def fused_kernel(
    hidden0, hidden1, queries0, queries1, key0, key1, value0, value1, table,
    gain0, gain1, documents0, documents1,
    out,
    gain_raw0, gain_raw1, doc_raw, near, rows, wide, normed, gain_send, gain_rows, row_send, row_data, query_rows, doc_wide,
    key_send, value_send, key_parts, value_parts, home, key_heads, value_heads, mixed, tables,
    ready, raw_sem, near_sem, table_sem, send_sem, row_sem, wide_sem, side_sem, gain_sem, data_sem, query_sem, part_sem, value_sem, out_sem,
):
    hiddens, queries = (hidden0, hidden1), (queries0, queries1)
    keys, values = (key0, key1), (value0, value1)
    tokens, features = hidden0.shape[1], key0.shape[0]
    slab = 8 * features
    head_cols = query_rows.shape[1]
    group_size = head_cols // HEAD_DIM
    length = query_rows.shape[0]
    sp, core, plane = lax.axis_index("sp"), lax.axis_index("fsdp"), lax.axis_index("groups")
    z, y = sp // 2, sp % 2
    upper, parity = z // 2, z % 2
    near_z = z + 1 - 2 * parity
    far_z = lax.rem(z + 2, 4)

    def scope(name):
        return jax.named_scope(name) if TRACE else contextlib.nullcontext()

    inner = upper != parity
    greeted = 6 + 2 * jnp.where(inner, 1, 0)

    def greet(semaphore):
        for c in range(2):
            pl.semaphore_signal(
                semaphore, inc=1, device_id={"groups": 1 - plane, "fsdp": c}, device_id_type=MESH
            )
            pl.semaphore_signal(
                semaphore, inc=1, device_id={"sp": near_z * 2 + y, "fsdp": c}, device_id_type=MESH
            )

            @pl.when(inner)
            def _(c=c):
                pl.semaphore_signal(
                    semaphore, inc=1, device_id={"sp": (3 - z) * 2 + y, "fsdp": c}, device_id_type=MESH
                )
        pl.semaphore_signal(semaphore, inc=1, device_id={"sp": z * 2 + 1 - y}, device_id_type=MESH)
        pl.semaphore_signal(semaphore, inc=1, device_id={"fsdp": 1 - core}, device_id_type=MESH)

    barrier = pltpu.get_barrier_semaphore()
    greet(barrier)

    def place(zz, yy, cc):
        return (zz * 2 + yy) * 2 + cc

    def place_rows(index):
        return pl.ds(pl.multiple_of(index * features, 128), features)

    mine = place(parity, y, core)
    own_any = (core == plane) & (core == parity)

    def columns(half, b):
        return pl.ds(pl.multiple_of((half * 2 + b) * HEAD_DIM, HEAD_DIM), HEAD_DIM)

    for m in range(2):
        pltpu.make_async_copy(hiddens[m].at[0], near.at[m], near_sem).start()
    small = (
        (gain0, gain_raw0), (gain1, gain_raw1), (documents0, doc_raw.at[0]), (documents1, doc_raw.at[1]),
    )
    for index, (src, dst) in enumerate(small):
        pltpu.make_async_copy(src, dst, raw_sem.at[index]).start()
    with scope("wbar"):
        pl.semaphore_wait(barrier, greeted)
    greet(ready.at[0])

    def next_round(step):
        with scope(f"wround{step}"):
            pl.semaphore_wait(ready.at[step], greeted)
        if step < 3:
            greet(ready.at[step + 1])

    def put(src, dst, recv, target, sent, away=None):
        def start():
            pltpu.make_async_remote_copy(
                src_ref=src, dst_ref=dst, send_sem=send_sem.at[sent], recv_sem=recv,
                device_id=target, device_id_type=MESH,
            ).start()

        if away is None:
            start()
        else:
            pl.when(away)(start)

    def send(src, dst, recv, target, sent, own):
        put(src, dst, recv, target, sent, jnp.logical_not(own))

        @pl.when(own)
        def _():
            pltpu.make_async_copy(src, dst, recv).start()

    def put_weight(b, half, target, sent, recv):
        for index, weights in enumerate((keys, values)):
            cols = slice(index * HEAD_DIM, (index + 1) * HEAD_DIM)
            for m in range(2):
                put(
                    weights[m].at[:, columns(half, b)], wide.at[b, place_rows(mine), cols], recv,
                    target, sent, plane == m,
                )

    def arrive(dst, recv, name):
        with scope(name):
            pltpu.make_async_copy(dst, dst, recv).wait()

    def lane(zz, yy):
        return zz * 2 + yy

    def forward(b, zz, yy, sent, further=None):
        block = wide.at[b, place_rows(place(zz, yy, core))]
        arrive(block, wide_sem.at[b, lane(zz, yy)], "wweight")
        put(block, block, side_sem.at[b], beside, sent)
        if further is not None:
            put(block, block, wide_sem.at[b, lane(zz, yy)], further, sent)

    def arrive_own(b):
        arrive(wide.at[b, place_rows(mine)], wide_sem.at[b, lane(parity, y)], "wown")

    def arrive_side(b):
        arrive(wide.at[b, :4 * features], side_sem.at[b], "wside")

    across, beside, along = {"sp": z * 2 + 1 - y}, {"fsdp": 1 - core}, {"sp": near_z * 2 + y}
    beyond = {"sp": near_z * 2 + 1 - y}
    away_head, home_head = 1 - upper, upper

    own_lane = lane(parity, y)
    put_weight(away_head, 1 - y, across, 0, wide_sem.at[away_head, own_lane])
    put_weight(away_head, y, along, 0, wide_sem.at[away_head, own_lane])
    put_weight(away_head, y, beside, 0, side_sem.at[away_head])
    put_weight(home_head, 1 - y, across, 0, wide_sem.at[home_head, own_lane])
    for m in range(2):
        @pl.when(plane == m)
        def _(m=m):
            for b in range(2):
                target = wide.at[b, place_rows(mine)]
                pltpu.make_async_copy(
                    keys[m].at[:, columns(y, b)], target.at[:, :HEAD_DIM], wide_sem.at[b, parity * 2 + y]
                ).start()
                pltpu.make_async_copy(
                    values[m].at[:, columns(y, b)], target.at[:, HEAD_DIM:], wide_sem.at[b, parity * 2 + y]
                ).start()

    pltpu.make_async_copy(table, tables, table_sem).start()
    pltpu.make_async_copy(near, near, near_sem).wait()

    def put_hidden(h, other, when=None):
        to_z = 2 * h + core
        m = 1 - plane if other else plane
        src, dst = near.at[m, :, pl.ds(pl.multiple_of(h * slab, 128), slab)], rows.at[sp]
        target = {"groups": m, "sp": to_z * 2 + y, "fsdp": plane}
        if other:
            put(src, dst, row_sem.at[sp], target, 2, when)
        else:
            own = (to_z == z) & (core == plane)
            send(src, dst, row_sem.at[sp], target, 2, own)

    for index, (src, dst) in enumerate(small):
        pltpu.make_async_copy(src, dst, raw_sem.at[index]).wait()
    put_hidden(upper, True, core == parity)
    square = (
        lax.broadcasted_iota(jnp.int32, (tokens, 128), 0)
        == lax.broadcasted_iota(jnp.int32, (tokens, 128), 1)
    )
    for m in range(2):
        wide_row = near[m].astype(jnp.float32)
        inverse = lax.rsqrt(jnp.mean(wide_row * wide_row, axis=-1, keepdims=True) + EPS)
        row_send[m] = jnp.sum(jnp.where(square, inverse, 0.0), axis=0, keepdims=True)
        row_send[m, :, 64:64 + tokens] = doc_raw[m].astype(jnp.float32)
    next_round(0)
    put_weight(away_head, 1 - y, beyond, 0, wide_sem.at[away_head, own_lane])
    gain_send[...] = jnp.where(
        plane == 0, gain_raw0[...].astype(jnp.float32), gain_raw1[...].astype(jnp.float32)
    ).reshape(1, -1)
    for zz in range(2):
        for yy in range(2):
            for cc in range(2):
                own = (parity == zz) & (y == yy) & (core == cc)
                send(
                    gain_send, gain_rows.at[mine], gain_sem,
                    {"sp": (upper * 2 + zz) * 2 + yy, "fsdp": cc}, 3, own,
                )
    put_hidden(upper, False)

    def put_queries():
        token_rows = pl.ds(pl.multiple_of(sp * tokens, 16), tokens)
        for m in range(2):
            for yy in range(2):
                for h in range(2):
                    to_z, head = 2 * h + core, yy * 2 + h
                    send(
                        queries[m].at[0, :, head * head_cols:(head + 1) * head_cols],
                        query_rows.at[token_rows], query_sem.at[upper],
                        {"groups": m, "sp": to_z * 2 + yy, "fsdp": plane}, 5,
                        (plane == m) & (y == yy) & (to_z == z) & (core == plane),
                    )

    def put_row_data(h):
        to_z = 2 * h + core
        for m in range(2):
            for yy in range(2):
                send(
                    row_send.at[m], row_data.at[sp], data_sem.at[upper],
                    {"groups": m, "sp": to_z * 2 + yy, "fsdp": plane}, 4,
                    (plane == m) & (y == yy) & (to_z == z) & (core == plane),
                )

    next_round(1)
    put_row_data(upper)
    put_hidden(upper, True, core != parity)
    put_hidden(1 - upper, False)
    next_round(2)
    next_round(3)
    put_row_data(1 - upper)
    put_hidden(1 - upper, True)
    put_queries()
    put_weight(home_head, y, along, 1, wide_sem.at[home_head, own_lane])
    put_weight(home_head, y, beside, 1, side_sem.at[home_head])


    def pass_rows(step):
        from_z = order[step]
        block = from_z * 2 + y
        arrive(rows.at[block], row_sem.at[block], f"whid{step}")
        put(rows.at[block], rows.at[block], row_sem.at[block], across, 6)

    order = (z, near_z + upper * (1 - near_z), 2 * (1 - upper), 3 + upper * (near_z - 3))
    pass_rows(0)
    forward(away_head, parity, 1 - y, 0)
    forward(away_head, 1 - parity, y, 0)
    forward(away_head, 1 - parity, 1 - y, 0)
    forward(home_head, parity, 1 - y, 1, along)
    pass_rows(1)
    pass_rows(2)
    arrive(gain_rows, gain_sem, "wgain")
    arrive_own(away_head)
    arrive_side(away_head)
    gain_row = jnp.concatenate([gain_rows[s] for s in range(8)], axis=1)
    partner = {"sp": far_z * 2 + y}

    def block_of(index, k):
        return index // 2 * 4 + 2 * k + (y if index % 2 == 0 else 1 - y)

    def project(index):
        if index % 2 == 0:
            arrive(row_data.at[2 * index:2 * index + 4], data_sem.at[index // 2], f"wdata{index}")
        for k in range(2):
            s = block_of(index, k)
            scale = jnp.sum(jnp.where(square, row_data[s], 0.0), axis=1, keepdims=True)
            spot = (index % 2 * 2 + k) * tokens
            normed[index // 2, spot:spot + tokens, :] = (
                rows[s].astype(jnp.float32) * scale * gain_row
            ).astype(jnp.bfloat16)
        spot = index % 2 * 2 * tokens
        part = jnp.dot(
            normed[index // 2, spot:spot + 2 * tokens, :], wide[away_head], preferred_element_type=jnp.float32
        )
        key_send[index] = part[:, :HEAD_DIM]
        value_send[index] = part[:, HEAD_DIM:].astype(jnp.bfloat16)
        put(key_send.at[index], key_parts.at[index], part_sem.at[index // 2], partner, 7)
        put(value_send.at[index], value_parts.at[index], value_sem.at[index // 2], partner, 8)

    def arrive_rows(index):
        for k in range(2):
            block = block_of(index, k)
            arrive(rows.at[block], row_sem.at[block], f"wfwd{index}")

    project(0)
    pass_rows(3)
    arrive_rows(1)
    project(1)
    project(2)
    shifted = (
        lax.broadcasted_iota(jnp.int32, (tokens, 128), 0) + 64
        == lax.broadcasted_iota(jnp.int32, (tokens, 128), 1)
    )
    for s in range(8):
        column = jnp.sum(jnp.where(shifted, row_data[s], 0.0), axis=1, keepdims=True)
        doc_wide[s * tokens:(s + 1) * tokens, :] = jnp.broadcast_to(column, (tokens, 128))
    query_index = lax.broadcasted_iota(jnp.int32, (length, length), 0)
    key_index = lax.broadcasted_iota(jnp.int32, (length, length), 1)
    doc_column = doc_wide[:, :1]
    doc_row = jnp.sum(jnp.where(query_index == key_index, doc_column, 0.0), axis=0, keepdims=True)
    forward(home_head, 1 - parity, y, 1)

    @pl.when(core != plane)
    def _():
        forward(home_head, 1 - parity, 1 - y, 1)

    arrive_rows(3)
    project(3)

    @pl.when(core == plane)
    def _():
        forward(home_head, 1 - parity, 1 - y, 1)

    arrive(tables, table_sem, "wtable")
    arrive_own(home_head)

    def home_part(half, c):
        total = None
        for index in range(4):
            at = place_rows(index * 2 + c)
            part = jnp.dot(normed[half, :, at], wide[home_head, at, :], preferred_element_type=jnp.float32)
            total = part if total is None else total + part
        return total

    for half in range(2):
        home[half] = home_part(half, core)
    arrive_side(home_head)

    factor = HEAD_DIM ** (-0.5)
    head = y * 2 + upper
    out_columns = pl.ds(pl.multiple_of(head * head_cols, 128), head_cols)
    half_rows = length // 2
    for half in range(2):
        whole = home[half] + home_part(half, 1 - core)
        arrive(key_parts.at[2 * half:2 * half + 2], part_sem.at[half], f"wpart{half}")
        arrive(value_parts.at[2 * half:2 * half + 2], value_sem.at[half], f"wpart{half}")
        for index in range(2 * half, 2 * half + 2):
            for k in range(2):
                block = pl.ds(pl.multiple_of(block_of(index, k) * tokens, 16), tokens)
                near_rows = slice(k * tokens, (k + 1) * tokens)
                spot = (index % 2 * 2 + k) * tokens
                raw_keys = whole[spot:spot + tokens, :HEAD_DIM] + key_parts[index, near_rows, :]
                raw_values = whole[spot:spot + tokens, HEAD_DIM:] + value_parts[index, near_rows, :].astype(jnp.float32)
                key_heads[block, :] = (
                    raw_keys * tables[0, block, :] + pltpu.roll(raw_keys, HEAD_DIM // 2, 1) * tables[1, block, :]
                ).astype(jnp.bfloat16)
                value_heads[block, :] = raw_values.astype(jnp.bfloat16)
        first, last = half * half_rows, (half + 1) * half_rows
        arrive(query_rows.at[first:last], query_sem.at[half], f"wq{half}")
        allowed = (
            lax.broadcasted_iota(jnp.int32, (half_rows, last), 1)
            <= first + lax.broadcasted_iota(jnp.int32, (half_rows, last), 0)
        ) & (doc_row[:, :last] == doc_wide[first:last, :1])
        for g in range(group_size):
            cols = slice(g * HEAD_DIM, (g + 1) * HEAD_DIM)
            scores = lax.dot_general(
                query_rows[first:last, cols], key_heads[:last, :], (((1,), (1,)), ((), ())),
                preferred_element_type=jnp.float32,
            ) * factor
            scores = jnp.where(allowed, scores, MASKED)
            highest = jnp.max(scores, axis=-1, keepdims=True)
            exponent = jnp.exp(scores - highest)
            weights = (exponent / jnp.sum(exponent, axis=-1, keepdims=True)).astype(jnp.bfloat16)
            mixed[half, :, cols] = jnp.dot(
                weights, value_heads[:last, :], preferred_element_type=jnp.float32
            ).astype(jnp.bfloat16)
        for k in range(4):
            to_sp = half * 4 + k
            send(
                mixed.at[half, k * tokens:(k + 1) * tokens], out.at[plane, 0, :, out_columns], out_sem,
                {"groups": core, "sp": to_sp, "fsdp": parity}, 9,
                (core == plane) & (sp == to_sp) & (core == parity),
            )
    def sent(ref, index):
        pltpu.make_async_copy(ref, ref, send_sem.at[index]).wait()

    with scope("wsend"):
        sent(wide.at[0], 0)
        sent(wide.at[1, :6 * features], 1)
        sent(gain_rows.at[:7], 3)
        sent(rows.at[:4], 6)
        sent(key_send, 7)
        sent(value_send, 8)
        for count in (7, 8):
            @pl.when(own_any if count == 7 else jnp.logical_not(own_any))
            def _(count=count):
                sent(rows.at[:count - 4], 2)
                sent(row_data.at[:count], 4)
                sent(query_rows.at[:count * tokens], 5)
                sent(query_rows.at[:count * tokens], 9)
    arrive(out, out_sem, "wout")


def fused(mesh, hiddens, queries, documents, gains, keys, values):
    sp = mesh.shape["sp"]
    tokens, features = hiddens[0].shape[1], keys[0].shape[0]
    kv_heads = keys[0].shape[1] // HEAD_DIM
    head_cols = queries[0].shape[2] // kv_heads
    length = sp * tokens
    half_dim = HEAD_DIM // 2
    frequency = ROPE_BASE ** (-2.0 * np.arange(half_dim) / HEAD_DIM)
    angles = np.arange(length)[:, None] * frequency[None, :]
    cosines = np.concatenate([np.cos(angles), np.cos(angles)], axis=1).astype(np.float32)
    sines = np.concatenate([-np.sin(angles), np.sin(angles)], axis=1).astype(np.float32)
    dma = pltpu.SemaphoreType.DMA
    bf16, f32 = jnp.bfloat16, jnp.float32
    out = pl.pallas_call(
        fused_kernel,
        out_shape=pltpu.VMEM((2, 1, tokens, queries[0].shape[2]), bf16),
        in_specs=[pl.BlockSpec(memory_space=pl.ANY)] * 13,
        out_specs=pl.BlockSpec(memory_space=pltpu.VMEM),
        scratch_shapes=[
            pltpu.VMEM((features,), bf16),
            pltpu.VMEM((features,), bf16),
            pltpu.VMEM((2, 1, tokens), jnp.int32),
            pltpu.VMEM((2,) + hiddens[0].shape[1:], bf16),
            pltpu.VMEM((sp, tokens, 8 * features), bf16),
            pltpu.VMEM((2, 8 * features, 2 * HEAD_DIM), bf16),
            pltpu.VMEM((2, 4 * tokens, 8 * features), bf16),
            pltpu.VMEM((1, features), f32),
            pltpu.VMEM((8, 1, features), f32),
            pltpu.VMEM((2, 1, 128), f32),
            pltpu.VMEM((sp, 1, 128), f32),
            pltpu.VMEM((length, head_cols), bf16),
            pltpu.VMEM((length, 128), f32),
            pltpu.VMEM((4, 2 * tokens, HEAD_DIM), f32),
            pltpu.VMEM((4, 2 * tokens, HEAD_DIM), bf16),
            pltpu.VMEM((4, 2 * tokens, HEAD_DIM), f32),
            pltpu.VMEM((4, 2 * tokens, HEAD_DIM), bf16),
            pltpu.VMEM((2, length // 2, 2 * HEAD_DIM), f32),
            pltpu.VMEM((length, HEAD_DIM), bf16),
            pltpu.VMEM((length, HEAD_DIM), bf16),
            pltpu.VMEM((2, length // 2, head_cols), bf16),
            pltpu.VMEM((2, length, HEAD_DIM), f32),
            pltpu.SemaphoreType.REGULAR((4,)),
            dma((4,)),
            dma(()),
            dma(()),
            dma((10,)),
            dma((sp,)),
            dma((2, 4)),
            dma((2,)),
            dma(()),
            dma((2,)),
            dma((2,)),
            dma((2,)),
            dma((2,)),
            dma(()),
        ],
        compiler_params=pltpu.CompilerParams(collective_id=0, has_side_effects=True),
        name="fused",
    )(
        *hiddens, *queries, *keys, *values, np.stack([cosines, sines]),
        *gains, *documents,
    )
    return out[0], out[1]


def per_device(
    mesh,
    policy_hidden,
    policy_queries,
    policy_documents,
    policy_gain,
    policy_key_weight,
    policy_value_weight,
    frozen_hidden,
    frozen_queries,
    frozen_documents,
    frozen_gain,
    frozen_key_weight,
    frozen_value_weight,
):
    if fits(mesh, policy_hidden, policy_queries, policy_key_weight):
        return fused(
            mesh,
            (policy_hidden, frozen_hidden),
            (policy_queries, frozen_queries),
            (policy_documents, frozen_documents),
            (policy_gain, frozen_gain),
            (policy_key_weight, frozen_key_weight),
            (policy_value_weight, frozen_value_weight),
        )
    policy_mixed = run_model(
        policy_hidden,
        policy_queries,
        policy_documents,
        policy_gain,
        policy_key_weight,
        policy_value_weight,
    )
    frozen_mixed = run_model(
        frozen_hidden,
        frozen_queries,
        frozen_documents,
        frozen_gain,
        frozen_key_weight,
        frozen_value_weight,
    )
    return (policy_mixed, frozen_mixed)


def solution(mesh):
    return jax.shard_map(
        functools.partial(per_device, mesh),
        mesh=mesh,
        in_specs=(
            P(("groups", "fsdp"), "sp", None),
            P(("groups", "fsdp"), "sp", None),
            P(("groups", "fsdp"), "sp"),
            P(("sp", "fsdp")),
            P(("sp", "fsdp"), None),
            P(("sp", "fsdp"), None),
            P(("groups", "fsdp"), "sp", None),
            P(("groups", "fsdp"), "sp", None),
            P(("groups", "fsdp"), "sp"),
            P(("sp", "fsdp")),
            P(("sp", "fsdp"), None),
            P(("sp", "fsdp"), None),
        ),
        out_specs=(P(("groups", "fsdp"), "sp", None), P(("groups", "fsdp"), "sp", None)),
        check_vma=False,
    )
```

time: 44.7 us -> 41.2 us (0.922)
  the two profiles are of different devices: /device:TPU:0 before, /device:TPU:1 now
where the time goes in v2:
time: 41.2 us; the launch traced here: 41.1 us
  Pallas kernels  39.8 us (97%)
  local copies, waits for them, and re-layouts  0.66 us (2%)
  between operations  0.64 us (2%)
    pallas_call x1, Pallas kernels, fused(): pl.pallas_call(fused_kernel, out_shape=pltpu.VMEM((2, 1, tokens, queries[...  39.8 us

profile of v2, /device:TPU:1, one launch (start us, length us, event | category | flops | bytes accessed | tf_op | source)
XLA Modules:
  0.0 41.1 jit_solution(17154303162180962095)
XLA Ops:
  0.6 39.8 %fused.1 = bf16[2,1,32,1024]{3,2,1,0:T(8,128)(2,1)S(1)} custom-call(bf16[1,32,4096]{2,1,0:T(8,128)(2,1)} %hidden0.1, bf16[1,32,4096]{2,1,0:T(8,128)(2,1)} %hidden1.1, bf16[1,32,1024]{2,1,0:T(8,128)(2,1)} %queries0.1, bf16[1,32,1024]{2,1,0:T(8,128)(2,1)} %queries1.1, bf16[256,512]{1,0:T(8,128)(2,1)} %key0.1, bf16[256,512]{1,0:T(8,128)(2,1)} %key1.1, ...), custom_call_target="tpu_custom_call" | custom-call | tf_op jit(solution)/shard_map/fused/pallas_call | solution.py:527
  40.4 0.7 %slice_bitcast_fusion = (bf16[1,32,1024]{2,1,0:T(8,128)(2,1)}, bf16[1,32,1024]{2,1,0:T(8,128)(2,1)}) fusion(bf16[2,1,32,1024]{3,2,1,0:T(8,128)(2,1)S(1)} %fused.1), kind=kLoop, calls=%fused_computation | loop fusion | bytes 262144 | tf_op jit(solution)/shard_map/squeeze | solution.py:576

commit v3 on v2

--- a/solution.py
+++ b/solution.py
@@ -158,24 +158,17 @@
         return jax.named_scope(name) if TRACE else contextlib.nullcontext()
 
     inner = upper != parity
-    greeted = 6 + 2 * jnp.where(inner, 1, 0)
+    greeted = 4 + jnp.where(inner, 1, 0)
 
     def greet(semaphore):
-        for c in range(2):
-            pl.semaphore_signal(
-                semaphore, inc=1, device_id={"groups": 1 - plane, "fsdp": c}, device_id_type=MESH
-            )
-            pl.semaphore_signal(
-                semaphore, inc=1, device_id={"sp": near_z * 2 + y, "fsdp": c}, device_id_type=MESH
-            )
-
-            @pl.when(inner)
-            def _(c=c):
-                pl.semaphore_signal(
-                    semaphore, inc=1, device_id={"sp": (3 - z) * 2 + y, "fsdp": c}, device_id_type=MESH
-                )
-        pl.semaphore_signal(semaphore, inc=1, device_id={"sp": z * 2 + 1 - y}, device_id_type=MESH)
-        pl.semaphore_signal(semaphore, inc=1, device_id={"fsdp": 1 - core}, device_id_type=MESH)
+        for target in (
+            {"sp": near_z * 2 + y}, {"sp": z * 2 + 1 - y}, {"groups": 1 - plane}, {"fsdp": 1 - core},
+        ):
+            pl.semaphore_signal(semaphore, inc=1, device_id=target, device_id_type=MESH)
+
+        @pl.when(inner)
+        def _():
+            pl.semaphore_signal(semaphore, inc=1, device_id={"sp": (3 - z) * 2 + y}, device_id_type=MESH)
 
     barrier = pltpu.get_barrier_semaphore()
     greet(barrier)
@@ -187,7 +180,7 @@
         return pl.ds(pl.multiple_of(index * features, 128), features)
 
     mine = place(parity, y, core)
-    own_any = (core == plane) & (core == parity)
+    leads = core == plane
 
     def columns(half, b):
         return pl.ds(pl.multiple_of((half * 2 + b) * HEAD_DIM, HEAD_DIM), HEAD_DIM)
@@ -206,7 +199,7 @@
     def next_round(step):
         with scope(f"wround{step}"):
             pl.semaphore_wait(ready.at[step], greeted)
-        if step < 3:
+        if step < 2:
             greet(ready.at[step + 1])
 
     def put(src, dst, recv, target, sent, away=None):
@@ -228,13 +221,13 @@
         def _():
             pltpu.make_async_copy(src, dst, recv).start()
 
-    def put_weight(b, half, target, sent, recv):
+    def put_weight(b, half, target, sent, recv, model, when=None):
         for index, weights in enumerate((keys, values)):
             cols = slice(index * HEAD_DIM, (index + 1) * HEAD_DIM)
             for m in range(2):
                 put(
                     weights[m].at[:, columns(half, b)], wide.at[b, place_rows(mine), cols], recv,
-                    target, sent, plane == m,
+                    target, sent, model == m if when is None else (model == m) & when,
                 )
 
     def arrive(dst, recv, name):
@@ -244,12 +237,11 @@
     def lane(zz, yy):
         return zz * 2 + yy
 
-    def forward(b, zz, yy, sent, further=None):
+    def forward(b, zz, yy):
         block = wide.at[b, place_rows(place(zz, yy, core))]
-        arrive(block, wide_sem.at[b, lane(zz, yy)], "wweight")
-        put(block, block, side_sem.at[b], beside, sent)
-        if further is not None:
-            put(block, block, wide_sem.at[b, lane(zz, yy)], further, sent)
+        arrive(block, wide_sem.at[b, lane(zz, yy)], ("wa" if b is away_head else "wh") + f"{1 if zz is parity else 0}{1 if yy is y else 0}")
+        put(block, block, wide_sem.at[b, lane(zz, yy)], {"groups": 1 - plane}, 1, leads)
+        put(block, block, side_sem.at[b], beside, 0)
 
     def arrive_own(b):
         arrive(wide.at[b, place_rows(mine)], wide_sem.at[b, lane(parity, y)], "wown")
@@ -262,98 +254,81 @@
     away_head, home_head = 1 - upper, upper
 
     own_lane = lane(parity, y)
-    put_weight(away_head, 1 - y, across, 0, wide_sem.at[away_head, own_lane])
-    put_weight(away_head, y, along, 0, wide_sem.at[away_head, own_lane])
-    put_weight(away_head, y, beside, 0, side_sem.at[away_head])
-    put_weight(home_head, 1 - y, across, 0, wide_sem.at[home_head, own_lane])
+
+    def put_weights(b, first):
+        recv = wide_sem.at[b, own_lane]
+        if first != 1:
+            put_weight(b, 1 - y, across, 1, recv, parity, leads)
+            put_weight(b, y, along, 1, recv, 1 - parity, leads)
+            put_weight(b, y, beside, 0, side_sem.at[b], parity)
+        if first != 0:
+            put_weight(b, 1 - y, beyond, 1, recv, 1 - parity, leads)
+
+    put_weights(away_head, 0)
     for m in range(2):
-        @pl.when(plane == m)
+        @pl.when(parity == m)
         def _(m=m):
             for b in range(2):
                 target = wide.at[b, place_rows(mine)]
                 pltpu.make_async_copy(
-                    keys[m].at[:, columns(y, b)], target.at[:, :HEAD_DIM], wide_sem.at[b, parity * 2 + y]
+                    keys[m].at[:, columns(y, b)], target.at[:, :HEAD_DIM], wide_sem.at[b, own_lane]
                 ).start()
                 pltpu.make_async_copy(
-                    values[m].at[:, columns(y, b)], target.at[:, HEAD_DIM:], wide_sem.at[b, parity * 2 + y]
+                    values[m].at[:, columns(y, b)], target.at[:, HEAD_DIM:], wide_sem.at[b, own_lane]
                 ).start()
 
     pltpu.make_async_copy(table, tables, table_sem).start()
     pltpu.make_async_copy(near, near, near_sem).wait()
 
-    def put_hidden(h, other, when=None):
-        to_z = 2 * h + core
-        m = 1 - plane if other else plane
-        src, dst = near.at[m, :, pl.ds(pl.multiple_of(h * slab, 128), slab)], rows.at[sp]
-        target = {"groups": m, "sp": to_z * 2 + y, "fsdp": plane}
-        if other:
-            put(src, dst, row_sem.at[sp], target, 2, when)
-        else:
-            own = (to_z == z) & (core == plane)
-            send(src, dst, row_sem.at[sp], target, 2, own)
-
+    def put_hidden(h, m):
+        src = near.at[m, :, pl.ds(pl.multiple_of(h * slab, 128), slab)]
+        put(src, rows.at[sp], row_sem.at[sp], {"sp": (2 * h + m) * 2 + y}, 2)
+
+    put_hidden(upper, 1 - parity)
+    pltpu.make_async_copy(
+        near.at[parity, :, pl.ds(pl.multiple_of(upper * slab, 128), slab)], rows.at[sp], row_sem.at[sp]
+    ).start()
+    next_round(0)
+    put_weights(away_head, 1)
+    first_far = jnp.where(inner, 1 - upper, upper)
+    put_hidden(1 - upper, first_far)
     for index, (src, dst) in enumerate(small):
         pltpu.make_async_copy(src, dst, raw_sem.at[index]).wait()
-    put_hidden(upper, True, core == parity)
     square = (
         lax.broadcasted_iota(jnp.int32, (tokens, 128), 0)
         == lax.broadcasted_iota(jnp.int32, (tokens, 128), 1)
     )
     for m in range(2):
+        gain_send[m] = (gain_raw0, gain_raw1)[m][...].astype(jnp.float32).reshape(1, -1)
         wide_row = near[m].astype(jnp.float32)
         inverse = lax.rsqrt(jnp.mean(wide_row * wide_row, axis=-1, keepdims=True) + EPS)
         row_send[m] = jnp.sum(jnp.where(square, inverse, 0.0), axis=0, keepdims=True)
         row_send[m, :, 64:64 + tokens] = doc_raw[m].astype(jnp.float32)
-    next_round(0)
-    put_weight(away_head, 1 - y, beyond, 0, wide_sem.at[away_head, own_lane])
-    gain_send[...] = jnp.where(
-        plane == 0, gain_raw0[...].astype(jnp.float32), gain_raw1[...].astype(jnp.float32)
-    ).reshape(1, -1)
-    for zz in range(2):
+    next_round(1)
+    put_hidden(1 - upper, 1 - first_far)
+    for m in range(2):
         for yy in range(2):
             for cc in range(2):
-                own = (parity == zz) & (y == yy) & (core == cc)
                 send(
-                    gain_send, gain_rows.at[mine], gain_sem,
-                    {"sp": (upper * 2 + zz) * 2 + yy, "fsdp": cc}, 3, own,
+                    gain_send.at[m], gain_rows.at[mine], gain_sem,
+                    {"sp": (upper * 2 + m) * 2 + yy, "fsdp": cc}, 3, (parity == m) & (y == yy) & (core == cc),
                 )
-    put_hidden(upper, False)
-
-    def put_queries():
-        token_rows = pl.ds(pl.multiple_of(sp * tokens, 16), tokens)
-        for m in range(2):
-            for yy in range(2):
-                for h in range(2):
-                    to_z, head = 2 * h + core, yy * 2 + h
-                    send(
-                        queries[m].at[0, :, head * head_cols:(head + 1) * head_cols],
-                        query_rows.at[token_rows], query_sem.at[upper],
-                        {"groups": m, "sp": to_z * 2 + yy, "fsdp": plane}, 5,
-                        (plane == m) & (y == yy) & (to_z == z) & (core == plane),
-                    )
-
-    def put_row_data(h):
-        to_z = 2 * h + core
-        for m in range(2):
-            for yy in range(2):
+    next_round(2)
+    token_rows = pl.ds(pl.multiple_of(sp * tokens, 16), tokens)
+    for m in range(2):
+        for yy in range(2):
+            for h in range(2):
+                to_sp = (2 * h + m) * 2 + yy
+                send(row_send.at[m], row_data.at[sp], data_sem.at[upper], {"sp": to_sp}, 4, sp == to_sp)
+    for m in range(2):
+        for yy in range(2):
+            for h in range(2):
+                to_sp, head = (2 * h + m) * 2 + yy, yy * 2 + h
                 send(
-                    row_send.at[m], row_data.at[sp], data_sem.at[upper],
-                    {"groups": m, "sp": to_z * 2 + yy, "fsdp": plane}, 4,
-                    (plane == m) & (y == yy) & (to_z == z) & (core == plane),
+                    queries[m].at[0, :, head * head_cols:(head + 1) * head_cols],
+                    query_rows.at[token_rows], query_sem.at[upper], {"sp": to_sp}, 5, sp == to_sp,
                 )
-
-    next_round(1)
-    put_row_data(upper)
-    put_hidden(upper, True, core != parity)
-    put_hidden(1 - upper, False)
-    next_round(2)
-    next_round(3)
-    put_row_data(1 - upper)
-    put_hidden(1 - upper, True)
-    put_queries()
-    put_weight(home_head, y, along, 1, wide_sem.at[home_head, own_lane])
-    put_weight(home_head, y, beside, 1, side_sem.at[home_head])
-
+    put_weights(home_head, 2)
 
     def pass_rows(step):
         from_z = order[step]
@@ -361,52 +336,71 @@
         arrive(rows.at[block], row_sem.at[block], f"whid{step}")
         put(rows.at[block], rows.at[block], row_sem.at[block], across, 6)
 
-    order = (z, near_z + upper * (1 - near_z), 2 * (1 - upper), 3 + upper * (near_z - 3))
+    order = (z, near_z, 3 * (1 - upper), 2 - upper)
+    def forward_all(b, *lanes):
+        for zz, yy in lanes:
+            forward(b, zz, yy)
+
+    side_lane, next_lane, last_lane = (parity, 1 - y), (1 - parity, y), (1 - parity, 1 - y)
+    follows = jnp.logical_not(leads)
+
+    def led(b, *lanes):
+        pl.when(leads)(lambda: forward_all(b, *lanes))
+
+    def followed(b, *lanes):
+        pl.when(follows)(lambda: forward_all(b, *lanes))
+
     pass_rows(0)
-    forward(away_head, parity, 1 - y, 0)
-    forward(away_head, 1 - parity, y, 0)
-    forward(away_head, 1 - parity, 1 - y, 0)
-    forward(home_head, parity, 1 - y, 1, along)
+    led(away_head, side_lane, next_lane)
     pass_rows(1)
-    pass_rows(2)
+    led(away_head, last_lane)
+    pl.when(follows)(lambda: pass_rows(2))
+    followed(away_head, side_lane, next_lane, last_lane)
+    pl.when(leads)(lambda: pass_rows(2))
+    pass_rows(3)
     arrive(gain_rows, gain_sem, "wgain")
     arrive_own(away_head)
     arrive_side(away_head)
     gain_row = jnp.concatenate([gain_rows[s] for s in range(8)], axis=1)
     partner = {"sp": far_z * 2 + y}
 
-    def block_of(index, k):
-        return index // 2 * 4 + 2 * k + (y if index % 2 == 0 else 1 - y)
-
-    def project(index):
-        if index % 2 == 0:
-            arrive(row_data.at[2 * index:2 * index + 4], data_sem.at[index // 2], f"wdata{index}")
+    def block_of(half, side, k):
+        return half * 4 + 2 * k + (y if side == 0 else 1 - y)
+
+    def project(half, side):
         for k in range(2):
-            s = block_of(index, k)
+            s = block_of(half, side, k)
             scale = jnp.sum(jnp.where(square, row_data[s], 0.0), axis=1, keepdims=True)
-            spot = (index % 2 * 2 + k) * tokens
-            normed[index // 2, spot:spot + tokens, :] = (
+            spot = (side * 2 + k) * tokens
+            normed[half, spot:spot + tokens, :] = (
                 rows[s].astype(jnp.float32) * scale * gain_row
             ).astype(jnp.bfloat16)
-        spot = index % 2 * 2 * tokens
+        spot = side * 2 * tokens
         part = jnp.dot(
-            normed[index // 2, spot:spot + 2 * tokens, :], wide[away_head], preferred_element_type=jnp.float32
+            normed[half, spot:spot + 2 * tokens, :], wide[away_head], preferred_element_type=jnp.float32
         )
+        index = half * 2 + side
         key_send[index] = part[:, :HEAD_DIM]
         value_send[index] = part[:, HEAD_DIM:].astype(jnp.bfloat16)
-        put(key_send.at[index], key_parts.at[index], part_sem.at[index // 2], partner, 7)
-        put(value_send.at[index], value_parts.at[index], value_sem.at[index // 2], partner, 8)
-
-    def arrive_rows(index):
+        put(key_send.at[index], key_parts.at[index], part_sem.at[half], partner, 7)
+        put(value_send.at[index], value_parts.at[index], value_sem.at[half], partner, 8)
+
+    def arrive_data(half):
+        arrive(row_data.at[pl.ds(4 * half, 4)], data_sem.at[half], "wdata")
+
+    def arrive_rows(half):
         for k in range(2):
-            block = block_of(index, k)
-            arrive(rows.at[block], row_sem.at[block], f"wfwd{index}")
-
-    project(0)
-    pass_rows(3)
-    arrive_rows(1)
-    project(1)
-    project(2)
+            block = block_of(half, 1, k)
+            arrive(rows.at[block], row_sem.at[block], "wfwd")
+
+    arrive_data(upper)
+    project(upper, 0)
+    arrive_rows(upper)
+    project(upper, 1)
+    led(home_head, side_lane, next_lane)
+    arrive_data(1 - upper)
+    project(1 - upper, 0)
+    led(home_head, last_lane)
     shifted = (
         lax.broadcasted_iota(jnp.int32, (tokens, 128), 0) + 64
         == lax.broadcasted_iota(jnp.int32, (tokens, 128), 1)
@@ -418,19 +412,9 @@
     key_index = lax.broadcasted_iota(jnp.int32, (length, length), 1)
     doc_column = doc_wide[:, :1]
     doc_row = jnp.sum(jnp.where(query_index == key_index, doc_column, 0.0), axis=0, keepdims=True)
-    forward(home_head, 1 - parity, y, 1)
-
-    @pl.when(core != plane)
-    def _():
-        forward(home_head, 1 - parity, 1 - y, 1)
-
-    arrive_rows(3)
-    project(3)
-
-    @pl.when(core == plane)
-    def _():
-        forward(home_head, 1 - parity, 1 - y, 1)
-
+    arrive_rows(1 - upper)
+    project(1 - upper, 1)
+    followed(home_head, side_lane, next_lane, last_lane)
     arrive(tables, table_sem, "wtable")
     arrive_own(home_head)
 
@@ -456,7 +440,7 @@
         arrive(value_parts.at[2 * half:2 * half + 2], value_sem.at[half], f"wpart{half}")
         for index in range(2 * half, 2 * half + 2):
             for k in range(2):
-                block = pl.ds(pl.multiple_of(block_of(index, k) * tokens, 16), tokens)
+                block = pl.ds(pl.multiple_of(block_of(half, index % 2, k) * tokens, 16), tokens)
                 near_rows = slice(k * tokens, (k + 1) * tokens)
                 spot = (index % 2 * 2 + k) * tokens
                 raw_keys = whole[spot:spot + tokens, :HEAD_DIM] + key_parts[index, near_rows, :]
@@ -487,27 +471,27 @@
         for k in range(4):
             to_sp = half * 4 + k
             send(
-                mixed.at[half, k * tokens:(k + 1) * tokens], out.at[plane, 0, :, out_columns], out_sem,
-                {"groups": core, "sp": to_sp, "fsdp": parity}, 9,
-                (core == plane) & (sp == to_sp) & (core == parity),
+                mixed.at[half, k * tokens:(k + 1) * tokens], out.at[parity, 0, :, out_columns], out_sem,
+                {"sp": to_sp}, 9, sp == to_sp,
             )
     def sent(ref, index):
         pltpu.make_async_copy(ref, ref, send_sem.at[index]).wait()
 
     with scope("wsend"):
         sent(wide.at[0], 0)
-        sent(wide.at[1, :6 * features], 1)
+
+        @pl.when(leads)
+        def _():
+            sent(wide.at[:, :6 * features], 1)
+
+        sent(rows.at[:3], 2)
         sent(gain_rows.at[:7], 3)
+        sent(row_data.at[:7], 4)
+        sent(query_rows.at[:7 * tokens], 5)
         sent(rows.at[:4], 6)
         sent(key_send, 7)
         sent(value_send, 8)
-        for count in (7, 8):
-            @pl.when(own_any if count == 7 else jnp.logical_not(own_any))
-            def _(count=count):
-                sent(rows.at[:count - 4], 2)
-                sent(row_data.at[:count], 4)
-                sent(query_rows.at[:count * tokens], 5)
-                sent(query_rows.at[:count * tokens], 9)
+        sent(query_rows.at[:7 * tokens], 9)
     arrive(out, out_sem, "wout")
 
 
@@ -537,7 +521,7 @@
             pltpu.VMEM((sp, tokens, 8 * features), bf16),
             pltpu.VMEM((2, 8 * features, 2 * HEAD_DIM), bf16),
             pltpu.VMEM((2, 4 * tokens, 8 * features), bf16),
-            pltpu.VMEM((1, features), f32),
+            pltpu.VMEM((2, 1, features), f32),
             pltpu.VMEM((8, 1, features), f32),
             pltpu.VMEM((2, 1, 128), f32),
             pltpu.VMEM((sp, 1, 128), f32),
@@ -552,7 +536,7 @@
             pltpu.VMEM((length, HEAD_DIM), bf16),
             pltpu.VMEM((2, length // 2, head_cols), bf16),
             pltpu.VMEM((2, length, HEAD_DIM), f32),
-            pltpu.SemaphoreType.REGULAR((4,)),
+            pltpu.SemaphoreType.REGULAR((3,)),
             dma((4,)),
             dma(()),
             dma(()),

time: 41.2 us -> 37.8 us (0.917)
  the two profiles are of different devices: /device:TPU:1 before, /device:TPU:26 now
where the time goes in v3:
time: 37.8 us; the launch traced here: 37.7 us
  Pallas kernels  36.4 us (96%)
  local copies, waits for them, and re-layouts  0.66 us (2%)
  between operations  0.64 us (2%)
    pallas_call x1, Pallas kernels, fused(): pl.pallas_call(fused_kernel, out_shape=pltpu.VMEM((2, 1, tokens, queries[...  36.4 us

profile of v3, /device:TPU:26, one launch (start us, length us, event | category | flops | bytes accessed | tf_op | source)
XLA Modules:
  0.0 37.7 jit_solution(4626776391575916149)
XLA Ops:
  0.6 36.4 %fused.1 = bf16[2,1,32,1024]{3,2,1,0:T(8,128)(2,1)S(1)} custom-call(bf16[1,32,4096]{2,1,0:T(8,128)(2,1)} %hidden0.1, bf16[1,32,4096]{2,1,0:T(8,128)(2,1)} %hidden1.1, bf16[1,32,1024]{2,1,0:T(8,128)(2,1)} %queries0.1, bf16[1,32,1024]{2,1,0:T(8,128)(2,1)} %queries1.1, bf16[256,512]{1,0:T(8,128)(2,1)} %key0.1, bf16[256,512]{1,0:T(8,128)(2,1)} %key1.1, ...), custom_call_target="tpu_custom_call" | custom-call | tf_op jit(solution)/shard_map/fused/pallas_call | solution.py:511
  37.0 0.7 %slice_bitcast_fusion = (bf16[1,32,1024]{2,1,0:T(8,128)(2,1)}, bf16[1,32,1024]{2,1,0:T(8,128)(2,1)}) fusion(bf16[2,1,32,1024]{3,2,1,0:T(8,128)(2,1)S(1)} %fused.1), kind=kLoop, calls=%fused_computation | loop fusion | bytes 262144 | tf_op jit(solution)/shard_map/squeeze | solution.py:560

commit v4 on v3

--- a/solution.py
+++ b/solution.py
@@ -180,7 +180,7 @@
         return pl.ds(pl.multiple_of(index * features, 128), features)
 
     mine = place(parity, y, core)
-    leads = core == plane
+    leads, follows = core == plane, core != plane
 
     def columns(half, b):
         return pl.ds(pl.multiple_of((half * 2 + b) * HEAD_DIM, HEAD_DIM), HEAD_DIM)
@@ -237,10 +237,11 @@
     def lane(zz, yy):
         return zz * 2 + yy
 
-    def forward(b, zz, yy):
+    def forward(b, zz, yy, onward):
         block = wide.at[b, place_rows(place(zz, yy, core))]
         arrive(block, wide_sem.at[b, lane(zz, yy)], ("wa" if b is away_head else "wh") + f"{1 if zz is parity else 0}{1 if yy is y else 0}")
-        put(block, block, wide_sem.at[b, lane(zz, yy)], {"groups": 1 - plane}, 1, leads)
+        if onward:
+            put(block, block, wide_sem.at[b, lane(zz, yy)], {"groups": 1 - plane}, 1)
         put(block, block, side_sem.at[b], beside, 0)
 
     def arrive_own(b):
@@ -255,16 +256,16 @@
 
     own_lane = lane(parity, y)
 
-    def put_weights(b, first):
+    def put_weights(b, lead, first):
         recv = wide_sem.at[b, own_lane]
         if first != 1:
-            put_weight(b, 1 - y, across, 1, recv, parity, leads)
-            put_weight(b, y, along, 1, recv, 1 - parity, leads)
+            put_weight(b, 1 - y, across, 1, recv, parity, lead)
+            put_weight(b, y, along, 1, recv, 1 - parity, lead)
             put_weight(b, y, beside, 0, side_sem.at[b], parity)
         if first != 0:
-            put_weight(b, 1 - y, beyond, 1, recv, 1 - parity, leads)
-
-    put_weights(away_head, 0)
+            put_weight(b, 1 - y, beyond, 1, recv, 1 - parity, lead)
+
+    put_weights(away_head, leads, 0)
     for m in range(2):
         @pl.when(parity == m)
         def _(m=m):
@@ -284,13 +285,14 @@
         src = near.at[m, :, pl.ds(pl.multiple_of(h * slab, 128), slab)]
         put(src, rows.at[sp], row_sem.at[sp], {"sp": (2 * h + m) * 2 + y}, 2)
 
-    put_hidden(upper, 1 - parity)
-    pltpu.make_async_copy(
-        near.at[parity, :, pl.ds(pl.multiple_of(upper * slab, 128), slab)], rows.at[sp], row_sem.at[sp]
-    ).start()
+    own_rows = near.at[parity, :, pl.ds(pl.multiple_of(upper * slab, 128), slab)]
+    put(own_rows, rows.at[sp], row_sem.at[sp], across, 6)
+    pl.when(follows)(lambda: put_hidden(upper, 1 - parity))
+    pltpu.make_async_copy(own_rows, rows.at[sp], row_sem.at[sp]).start()
     next_round(0)
-    put_weights(away_head, 1)
-    first_far = jnp.where(inner, 1 - upper, upper)
+    put_weights(away_head, leads, 1)
+    pl.when(leads)(lambda: put_hidden(upper, 1 - parity))
+    first_far = jnp.where(inner & leads, 1 - upper, upper)
     put_hidden(1 - upper, first_far)
     for index, (src, dst) in enumerate(small):
         pltpu.make_async_copy(src, dst, raw_sem.at[index]).wait()
@@ -320,6 +322,7 @@
             for h in range(2):
                 to_sp = (2 * h + m) * 2 + yy
                 send(row_send.at[m], row_data.at[sp], data_sem.at[upper], {"sp": to_sp}, 4, sp == to_sp)
+    pl.when(inner)(lambda: put_weights(home_head, leads, 2))
     for m in range(2):
         for yy in range(2):
             for h in range(2):
@@ -328,7 +331,7 @@
                     queries[m].at[0, :, head * head_cols:(head + 1) * head_cols],
                     query_rows.at[token_rows], query_sem.at[upper], {"sp": to_sp}, 5, sp == to_sp,
                 )
-    put_weights(home_head, 2)
+    pl.when(jnp.logical_not(inner))(lambda: put_weights(home_head, leads, 2))
 
     def pass_rows(step):
         from_z = order[step]
@@ -337,27 +340,28 @@
         put(rows.at[block], rows.at[block], row_sem.at[block], across, 6)
 
     order = (z, near_z, 3 * (1 - upper), 2 - upper)
-    def forward_all(b, *lanes):
+    def forward_all(b, onward, *lanes):
         for zz, yy in lanes:
-            forward(b, zz, yy)
+            forward(b, zz, yy, onward)
 
     side_lane, next_lane, last_lane = (parity, 1 - y), (1 - parity, y), (1 - parity, 1 - y)
-    follows = jnp.logical_not(leads)
-
-    def led(b, *lanes):
-        pl.when(leads)(lambda: forward_all(b, *lanes))
-
-    def followed(b, *lanes):
-        pl.when(follows)(lambda: forward_all(b, *lanes))
-
-    pass_rows(0)
-    led(away_head, side_lane, next_lane)
+
+    def led(b, lead, *lanes):
+        pl.when(lead)(lambda: forward_all(b, True, *lanes))
+
+    def followed(b, lead, *lanes):
+        pl.when(jnp.logical_not(lead))(lambda: forward_all(b, False, *lanes))
+
+    arrive(rows.at[sp], row_sem.at[sp], "whid0")
+    led(away_head, leads, side_lane, next_lane)
     pass_rows(1)
-    led(away_head, last_lane)
+    led(away_head, leads, last_lane)
     pl.when(follows)(lambda: pass_rows(2))
-    followed(away_head, side_lane, next_lane, last_lane)
+    followed(away_head, leads, side_lane, next_lane)
     pl.when(leads)(lambda: pass_rows(2))
     pass_rows(3)
+    followed(away_head, leads, last_lane)
+    led(home_head, leads, side_lane, next_lane)
     arrive(gain_rows, gain_sem, "wgain")
     arrive_own(away_head)
     arrive_side(away_head)
@@ -397,10 +401,9 @@
     project(upper, 0)
     arrive_rows(upper)
     project(upper, 1)
-    led(home_head, side_lane, next_lane)
+    led(home_head, leads, last_lane)
     arrive_data(1 - upper)
     project(1 - upper, 0)
-    led(home_head, last_lane)
     shifted = (
         lax.broadcasted_iota(jnp.int32, (tokens, 128), 0) + 64
         == lax.broadcasted_iota(jnp.int32, (tokens, 128), 1)
@@ -412,9 +415,10 @@
     key_index = lax.broadcasted_iota(jnp.int32, (length, length), 1)
     doc_column = doc_wide[:, :1]
     doc_row = jnp.sum(jnp.where(query_index == key_index, doc_column, 0.0), axis=0, keepdims=True)
+    followed(home_head, leads, side_lane, next_lane)
     arrive_rows(1 - upper)
     project(1 - upper, 1)
-    followed(home_head, side_lane, next_lane, last_lane)
+    followed(home_head, leads, last_lane)
     arrive(tables, table_sem, "wtable")
     arrive_own(home_head)
 
@@ -434,10 +438,21 @@
     head = y * 2 + upper
     out_columns = pl.ds(pl.multiple_of(head * head_cols, 128), head_cols)
     half_rows = length // 2
+
+    def put_out(half):
+        for k in range(4):
+            to_sp = half * 4 + k
+            send(
+                mixed.at[half, k * tokens:(k + 1) * tokens], out.at[parity, 0, :, out_columns], out_sem,
+                {"sp": to_sp}, 9, sp == to_sp,
+            )
+
     for half in range(2):
         whole = home[half] + home_part(half, 1 - core)
         arrive(key_parts.at[2 * half:2 * half + 2], part_sem.at[half], f"wpart{half}")
         arrive(value_parts.at[2 * half:2 * half + 2], value_sem.at[half], f"wpart{half}")
+        if half:
+            pl.when(upper == 1)(lambda: put_out(0))
         for index in range(2 * half, 2 * half + 2):
             for k in range(2):
                 block = pl.ds(pl.multiple_of(block_of(half, index % 2, k) * tokens, 16), tokens)
@@ -455,30 +470,30 @@
             lax.broadcasted_iota(jnp.int32, (half_rows, last), 1)
             <= first + lax.broadcasted_iota(jnp.int32, (half_rows, last), 0)
         ) & (doc_row[:, :last] == doc_wide[first:last, :1])
+        stacked = jnp.concatenate(
+            [query_rows[first:last, g * HEAD_DIM:(g + 1) * HEAD_DIM] for g in range(group_size)], axis=0
+        )
+        scores = lax.dot_general(
+            stacked, key_heads[:last, :], (((1,), (1,)), ((), ())), preferred_element_type=jnp.float32
+        ) * factor
+        scores = jnp.where(jnp.concatenate([allowed] * group_size, axis=0), scores, MASKED)
+        highest = jnp.max(scores, axis=-1, keepdims=True)
+        exponent = jnp.exp(scores - highest)
+        weights = (exponent / jnp.sum(exponent, axis=-1, keepdims=True)).astype(jnp.bfloat16)
+        blended = jnp.dot(weights, value_heads[:last, :], preferred_element_type=jnp.float32).astype(jnp.bfloat16)
         for g in range(group_size):
-            cols = slice(g * HEAD_DIM, (g + 1) * HEAD_DIM)
-            scores = lax.dot_general(
-                query_rows[first:last, cols], key_heads[:last, :], (((1,), (1,)), ((), ())),
-                preferred_element_type=jnp.float32,
-            ) * factor
-            scores = jnp.where(allowed, scores, MASKED)
-            highest = jnp.max(scores, axis=-1, keepdims=True)
-            exponent = jnp.exp(scores - highest)
-            weights = (exponent / jnp.sum(exponent, axis=-1, keepdims=True)).astype(jnp.bfloat16)
-            mixed[half, :, cols] = jnp.dot(
-                weights, value_heads[:last, :], preferred_element_type=jnp.float32
-            ).astype(jnp.bfloat16)
-        for k in range(4):
-            to_sp = half * 4 + k
-            send(
-                mixed.at[half, k * tokens:(k + 1) * tokens], out.at[parity, 0, :, out_columns], out_sem,
-                {"sp": to_sp}, 9, sp == to_sp,
-            )
+            mixed[half, :, g * HEAD_DIM:(g + 1) * HEAD_DIM] = blended[g * half_rows:(g + 1) * half_rows, :]
+        if half:
+            put_out(1)
+        else:
+            pl.when(upper == 0)(lambda: put_out(0))
+
     def sent(ref, index):
         pltpu.make_async_copy(ref, ref, send_sem.at[index]).wait()
 
     with scope("wsend"):
         sent(wide.at[0], 0)
+
 
         @pl.when(leads)
         def _():

time: 37.8 us -> 36.4 us (0.963)
  the two profiles are of different devices: /device:TPU:26 before, /device:TPU:0 now
where the time goes in v4:
time: 36.4 us; the launch traced here: 36.3 us
  Pallas kernels  35 us (96%)
  local copies, waits for them, and re-layouts  0.66 us (2%)
  between operations  0.64 us (2%)
    pallas_call x1, Pallas kernels, fused(): pl.pallas_call(fused_kernel, out_shape=pltpu.VMEM((2, 1, tokens, queries[...  35 us

profile of v4, /device:TPU:0, one launch (start us, length us, event | category | flops | bytes accessed | tf_op | source)
XLA Modules:
  0.0 36.3 jit_solution(17532399163746234165)
XLA Ops:
  0.6 35.0 %fused.1 = bf16[2,1,32,1024]{3,2,1,0:T(8,128)(2,1)S(1)} custom-call(bf16[1,32,4096]{2,1,0:T(8,128)(2,1)} %hidden0.1, bf16[1,32,4096]{2,1,0:T(8,128)(2,1)} %hidden1.1, bf16[1,32,1024]{2,1,0:T(8,128)(2,1)} %queries0.1, bf16[1,32,1024]{2,1,0:T(8,128)(2,1)} %queries1.1, bf16[256,512]{1,0:T(8,128)(2,1)} %key0.1, bf16[256,512]{1,0:T(8,128)(2,1)} %key1.1, ...), custom_call_target="tpu_custom_call" | custom-call | tf_op jit(solution)/shard_map/fused/pallas_call | solution.py:526
  35.6 0.7 %slice_bitcast_fusion = (bf16[1,32,1024]{2,1,0:T(8,128)(2,1)}, bf16[1,32,1024]{2,1,0:T(8,128)(2,1)}) fusion(bf16[2,1,32,1024]{3,2,1,0:T(8,128)(2,1)S(1)} %fused.1), kind=kLoop, calls=%fused_computation | loop fusion | bytes 262144 | tf_op jit(solution)/shard_map/squeeze | solution.py:575

commit v5 on v4

--- a/solution.py
+++ b/solution.py
@@ -138,7 +138,7 @@
     gain0, gain1, documents0, documents1,
     out,
     gain_raw0, gain_raw1, doc_raw, near, rows, wide, normed, gain_send, gain_rows, row_send, row_data, query_rows, doc_wide,
-    key_send, value_send, key_parts, value_parts, home, key_heads, value_heads, mixed, tables,
+    key_send, value_send, key_parts, value_parts, bias, home, key_heads, value_heads, mixed, tables,
     ready, raw_sem, near_sem, table_sem, send_sem, row_sem, wide_sem, side_sem, gain_sem, data_sem, query_sem, part_sem, value_sem, out_sem,
 ):
     hiddens, queries = (hidden0, hidden1), (queries0, queries1)
@@ -415,6 +415,7 @@
     key_index = lax.broadcasted_iota(jnp.int32, (length, length), 1)
     doc_column = doc_wide[:, :1]
     doc_row = jnp.sum(jnp.where(query_index == key_index, doc_column, 0.0), axis=0, keepdims=True)
+    bias[...] = jnp.where((key_index <= query_index) & (doc_row == doc_column), 0.0, MASKED)
     followed(home_head, leads, side_lane, next_lane)
     arrive_rows(1 - upper)
     project(1 - upper, 1)
@@ -452,7 +453,7 @@
         arrive(key_parts.at[2 * half:2 * half + 2], part_sem.at[half], f"wpart{half}")
         arrive(value_parts.at[2 * half:2 * half + 2], value_sem.at[half], f"wpart{half}")
         if half:
-            pl.when(upper == 1)(lambda: put_out(0))
+            pl.when(z == 3)(lambda: put_out(0))
         for index in range(2 * half, 2 * half + 2):
             for k in range(2):
                 block = pl.ds(pl.multiple_of(block_of(half, index % 2, k) * tokens, 16), tokens)
@@ -466,17 +467,13 @@
                 value_heads[block, :] = raw_values.astype(jnp.bfloat16)
         first, last = half * half_rows, (half + 1) * half_rows
         arrive(query_rows.at[first:last], query_sem.at[half], f"wq{half}")
-        allowed = (
-            lax.broadcasted_iota(jnp.int32, (half_rows, last), 1)
-            <= first + lax.broadcasted_iota(jnp.int32, (half_rows, last), 0)
-        ) & (doc_row[:, :last] == doc_wide[first:last, :1])
         stacked = jnp.concatenate(
             [query_rows[first:last, g * HEAD_DIM:(g + 1) * HEAD_DIM] for g in range(group_size)], axis=0
         )
         scores = lax.dot_general(
             stacked, key_heads[:last, :], (((1,), (1,)), ((), ())), preferred_element_type=jnp.float32
         ) * factor
-        scores = jnp.where(jnp.concatenate([allowed] * group_size, axis=0), scores, MASKED)
+        scores = scores + jnp.concatenate([bias[first:last, :last]] * group_size, axis=0)
         highest = jnp.max(scores, axis=-1, keepdims=True)
         exponent = jnp.exp(scores - highest)
         weights = (exponent / jnp.sum(exponent, axis=-1, keepdims=True)).astype(jnp.bfloat16)
@@ -486,7 +483,7 @@
         if half:
             put_out(1)
         else:
-            pl.when(upper == 0)(lambda: put_out(0))
+            pl.when(z < 3)(lambda: put_out(0))
 
     def sent(ref, index):
         pltpu.make_async_copy(ref, ref, send_sem.at[index]).wait()
@@ -546,6 +543,7 @@
             pltpu.VMEM((4, 2 * tokens, HEAD_DIM), bf16),
             pltpu.VMEM((4, 2 * tokens, HEAD_DIM), f32),
             pltpu.VMEM((4, 2 * tokens, HEAD_DIM), bf16),
+            pltpu.VMEM((length, length), f32),
             pltpu.VMEM((2, length // 2, 2 * HEAD_DIM), f32),
             pltpu.VMEM((length, HEAD_DIM), bf16),
             pltpu.VMEM((length, HEAD_DIM), bf16),

time: 36.4 us -> 36.4 us (level)
  no operation moved by 1% of the time
where the time goes in v5:
time: 36.4 us; the launch traced here: 36.3 us
  Pallas kernels  35 us (96%)
  local copies, waits for them, and re-layouts  0.66 us (2%)
  between operations  0.64 us (2%)
    pallas_call x1, Pallas kernels, fused(): pl.pallas_call(fused_kernel, out_shape=pltpu.VMEM((2, 1, tokens, queries[...  35 us

profile of v5, /device:TPU:0, one launch (start us, length us, event | category | flops | bytes accessed | tf_op | source)
XLA Modules:
  0.0 36.3 jit_solution(2093643014331210083)
XLA Ops:
  0.6 35.0 %fused.1 = bf16[2,1,32,1024]{3,2,1,0:T(8,128)(2,1)S(1)} custom-call(bf16[1,32,4096]{2,1,0:T(8,128)(2,1)} %hidden0.1, bf16[1,32,4096]{2,1,0:T(8,128)(2,1)} %hidden1.1, bf16[1,32,1024]{2,1,0:T(8,128)(2,1)} %queries0.1, bf16[1,32,1024]{2,1,0:T(8,128)(2,1)} %queries1.1, bf16[256,512]{1,0:T(8,128)(2,1)} %key0.1, bf16[256,512]{1,0:T(8,128)(2,1)} %key1.1, ...), custom_call_target="tpu_custom_call" | custom-call | tf_op jit(solution)/shard_map/fused/pallas_call | solution.py:523
  35.6 0.7 %slice_bitcast_fusion = (bf16[1,32,1024]{2,1,0:T(8,128)(2,1)}, bf16[1,32,1024]{2,1,0:T(8,128)(2,1)}) fusion(bf16[2,1,32,1024]{3,2,1,0:T(8,128)(2,1)S(1)} %fused.1), kind=kLoop, calls=%fused_computation | loop fusion | bytes 262144 | tf_op jit(solution)/shard_map/squeeze | solution.py:573
